TPU v7x, 32 devices: a whole 2x2x4 slice. The times are simulated.
32 devices in a mesh: rep: 8 (over z, x), tp: 4 (over y, core).
Axes of the slice: x: 2, y: 2, z: 4, core: 2. Of those that a mesh axis runs over, the one named last changes fastest.
Arguments:
- prompt_queries: bfloat16 [3968, 4096], P('rep', 'tp'), parts along dimension 0, may hold values from -240 to 240
- prompt_entries: bfloat16 [16, 496, 512], P('rep', 'tp'), parts along dimension 0, may hold values from -6 to 6
- history_cache: bfloat16 [16, 1024, 512], P('rep', 'tp'), parts along dimension 0, may hold values from -6 to 6
- decode_queries: bfloat16 [128, 4096], P('rep', 'tp'), parts along dimension 0, may hold values from -240 to 240
- decode_entries: bfloat16 [16, 16, 512], P('rep'), parts along dimension 0, may hold values from -6 to 6
- decode_cache: bfloat16 [16, 16, 768, 512], P('rep', None, 'tp'), parts along dimension 0, may hold values from -6 to 6
- decode_lengths: int32 [128], P('rep'), parts along dimension 0, may hold values from 1 to 768
- prompt_start: int32 [8], P('rep'), parts along dimension 0, may hold values from 512 to 1024
- out_weight: bfloat16 [4096, 4096], P('tp'), may hold values from -0.09375 to 0.09375
- residual: bfloat16 [512, 32768], P('tp', 'rep'), parts along dimension 1, may hold values from -4 to 4
- norm_gain: float32 [4096], replicated, may hold values from 0.5 to 1.5
Outputs:
- new_residual: bfloat16 [512, 32768], P('tp', 'rep'), parts along dimension 1
- normed: bfloat16 [512, 32768], P('tp', 'rep'), parts along dimension 1
There are 8 independent parts, one for each index of `rep`. A program takes and returns all parts, laid end to end along the dimension named above; an argument that names none is the same for every part. Nothing has to cross between parts.
Inputs may be any that keep to these rules, and one draw needn't show every extreme that they name: The rows of history_cache at and past prompt_start are not read. `decode_lengths`: rows of decode_cache at and past a request's length are not read.
All inputs are finite; a program needn't handle non-finite values.
Results may differ from a plain program's by a relative error of at most 0.017.
Values may be sent and summed in bfloat16 or wider, within the bound.
No kernel may reach another device: no remote copies, remote signals or barrier semaphores. Data moves between devices by JAX's collectives and lax.ppermute only.
A program may use at most 64 MiB of HBM per device.

v0:
```python
import jax
import jax.numpy as jnp
import numpy as np
from jax import lax
from jax.experimental import pallas as pl
from jax.experimental.pallas import tpu as pltpu
from jax.sharding import PartitionSpec as P


HEAD_DIM = 128
MASKED = -1e30
EPS = 1e-05
CHUNKS = (64, 64)
COLUMNS = 512
FIRST_EIGHTHS = 3
GROUP_ROWS = 256

F32 = jnp.float32
BF16 = jnp.bfloat16


def round_up(value, unit):
    return -(-value // unit) * unit


def hbm():
    return pl.BlockSpec(memory_space=pl.ANY)


def in_hbm():
    return pl.BlockSpec(memory_space=pltpu.HBM)


def in_vmem():
    return pl.BlockSpec(memory_space=pltpu.VMEM)


def to_hbm(value):
    return pltpu.with_memory_space_constraint(value, pltpu.HBM)


def busy(us):
    return pl.CostEstimate(flops=us * 500_000_000, transcendentals=0, bytes_accessed=us * 1_000_000)


def params(mib, **kwargs):
    return pltpu.CompilerParams(vmem_limit_bytes=mib << 20, **kwargs)


def pack_history(history, queries, entries, slots, local_heads, group):
    h_rows = history.shape[1]
    rows = queries.shape[0]
    devices = len(slots)

    def body(h_hbm, q_hbm, e_hbm, *refs):
        o_refs, (q_ref, e_ref, sem) = refs[:devices], refs[devices:]
        me = lax.axis_index("tp")
        lane = pl.multiple_of(me * local_heads // group * HEAD_DIM, HEAD_DIM)
        copies = [pltpu.make_async_copy(e_hbm.at[:, :, pl.ds(lane, HEAD_DIM)], e_ref, sem.at[0])]
        for i, k in enumerate(slots):
            lane = pl.multiple_of((me ^ k) * local_heads // group * HEAD_DIM, HEAD_DIM)
            for part in range(2):
                copies.append(
                    pltpu.make_async_copy(
                        h_hbm.at[part, :, pl.ds(lane, HEAD_DIM)],
                        o_refs[i].at[part * h_rows : (part + 1) * h_rows, :],
                        sem.at[len(copies)],
                    )
                )
        for h in range(local_heads):
            copies.append(
                pltpu.make_async_copy(
                    q_hbm.at[:, h * HEAD_DIM : (h + 1) * HEAD_DIM],
                    q_ref.at[h * rows : (h + 1) * rows, :],
                    sem.at[len(copies)],
                )
            )
        for copy in copies:
            copy.start()
        for copy in copies:
            copy.wait()

    outs = pl.pallas_call(
        body,
        in_specs=[in_hbm()] * 3,
        out_specs=[in_vmem()] * (devices + 2),
        out_shape=[jax.ShapeDtypeStruct((2 * h_rows, HEAD_DIM), BF16)] * devices
        + [
            jax.ShapeDtypeStruct((rows * local_heads, HEAD_DIM), BF16),
            pltpu.VMEM((2, rows, HEAD_DIM), BF16),
        ],
        scratch_shapes=[pltpu.SemaphoreType.DMA((1 + 2 * devices + local_heads,))],
        compiler_params=params(2),
        cost_estimate=busy(6),
        name="pack_history",
    )(to_hbm(history), to_hbm(queries), to_hbm(entries))
    return dict(zip(slots, outs)), outs[devices], outs[devices + 1]


def pack_fresh(prompt, history, query, slots, local_heads, group):
    h_rows, p_rows = history.shape[0] // 2, prompt.shape[1]
    p_pad = round_up(p_rows, 16)
    every = [1] + slots
    n = len(every)

    def body(p_ref, h_ref, q_ref, *o_refs):
        me = lax.axis_index("tp")
        o_refs[0][0 : 2 * h_rows, :] = h_ref[...]
        for i, k in enumerate(every):
            lane = pl.multiple_of((me ^ k) * local_heads // group * HEAD_DIM, HEAD_DIM)
            row = 2 * h_rows if i == 0 else 0
            for part in range(2):
                fresh = p_ref[part, :, pl.ds(lane, HEAD_DIM)]
                if p_pad > p_rows:
                    fresh = jnp.concatenate(
                        [fresh.astype(F32), jnp.zeros((p_pad - p_rows, HEAD_DIM), F32)], axis=0
                    ).astype(BF16)
                o_refs[i][row + part * p_pad : row + (part + 1) * p_pad, :] = fresh
        o_refs[0][2 * (h_rows + p_pad) :, :] = q_ref[...]

    sizes = [2 * (h_rows + p_pad) + query.shape[0]] + [2 * p_pad] * len(slots)
    outs = pl.pallas_call(
        body,
        in_specs=[in_vmem()] * 3,
        out_specs=[in_vmem()] * n,
        out_shape=[jax.ShapeDtypeStruct((size, HEAD_DIM), BF16) for size in sizes],
        compiler_params=params(8),
        cost_estimate=busy(12),
        name="pack_fresh",
    )(prompt, history, query)
    return outs[0], dict(zip(slots, outs[1:]))


def split(value):
    terms = []
    for _ in range(3):
        terms.append(value.astype(BF16))
        value = value - terms[-1].astype(F32)
    return terms


def decode_partials(queries, bundle, cache, prompt_queries, limits, local_heads, group):
    devices = len(queries) + 1
    held = list(queries)
    rows, span, width = cache.shape[1], cache.shape[2], cache.shape[3]
    kv_heads = width // HEAD_DIM
    heads = devices * local_heads
    factor = HEAD_DIM ** (-0.5) * float(np.log2(np.e))
    part_rows = rows * local_heads
    stat_rows = round_up(local_heads, 8)
    prompt_rows, local_width = prompt_queries.shape

    def body(limits_ref, *refs):
        q_refs, refs = dict(zip(held, refs)), refs[devices - 1 :]
        bundle_ref, cache_ref, pq_ref = refs[:3]
        o_refs, refs = refs[3 : 3 + devices], refs[3 + devices :]
        q_ref, q_all, sums = refs
        me = lax.axis_index("tp")
        q_ref[0:prompt_rows, :] = pq_ref[...]
        q_ref[prompt_rows:, :] = jnp.zeros((rows, local_width), BF16)
        for k in range(devices):
            q_ref_k, base = (bundle_ref, bundle.shape[0] - part_rows) if k == 1 else (q_refs[k], 0)
            for h in range(local_heads):
                row = base + h * rows
                q_all[k, pl.ds(h, rows, stride=local_heads), :] = q_ref_k[row : row + rows, :].astype(F32)

        slot = lax.broadcasted_iota(jnp.int32, (heads, 1), 0) // local_heads
        reads = ((slot ^ me) * local_heads) // group
        lane = lax.broadcasted_iota(jnp.int32, (heads, HEAD_DIM), 1)
        place = me * span + lax.broadcasted_iota(jnp.int32, (1, span), 1)
        scores = []
        for b in range(rows):
            here = slice(b * local_heads, (b + 1) * local_heads)
            q = jnp.concatenate([q_all[k, here, :] for k in range(devices)], axis=0)
            spread = jnp.concatenate(
                [jnp.where(reads == g, q, 0.0) for g in range(kv_heads)], axis=1
            ).astype(BF16)
            score = lax.dot_general(
                spread, cache_ref[0, b], (((1,), (1,)), ((), ())), preferred_element_type=F32
            )
            scores.append(jnp.where(place < limits_ref[1 + b : 2 + b, 0:1], score, MASKED))
        scores = jnp.concatenate(scores, axis=0)
        top = jnp.max(scores, axis=-1, keepdims=True)
        weights = jnp.where(scores > 0.5 * MASKED, jnp.exp2((scores - top) * factor), 0.0)
        total = jnp.sum(weights, axis=-1, keepdims=True)
        weights = weights.astype(BF16)
        stats = jnp.zeros((heads, HEAD_DIM), F32)
        for b in range(rows):
            these = slice(b * heads, (b + 1) * heads)
            summed = jnp.dot(weights[these], cache_ref[1, b], preferred_element_type=F32)
            own = jnp.zeros((heads, HEAD_DIM), F32)
            for g in range(kv_heads):
                own = own + jnp.where(reads == g, summed[:, g * HEAD_DIM : (g + 1) * HEAD_DIM], 0.0)
            for k in range(devices):
                sums[k, b * local_heads : (b + 1) * local_heads, :] = own[k * local_heads : (k + 1) * local_heads]
            stats = jnp.where(lane == b, top[these], jnp.where(lane == rows + b, total[these], stats))
        terms = split(stats)
        for k in range(devices):
            o_refs[k][0:part_rows, :] = sums[k].astype(BF16)
            for i, term in enumerate(terms):
                row = part_rows + i * stat_rows
                o_refs[k][row : row + local_heads, :] = term[k * local_heads : (k + 1) * local_heads, :]

    outs = pl.pallas_call(
        body,
        in_specs=[in_vmem()] * (devices + 3),
        out_specs=[in_vmem()] * (devices + 1),
        scratch_shapes=[pltpu.VMEM((devices, part_rows, HEAD_DIM), F32)] * 2,
        out_shape=[jax.ShapeDtypeStruct((part_rows + 3 * stat_rows, HEAD_DIM), BF16)] * devices
        + [pltpu.VMEM((prompt_rows + rows, local_width), BF16)],
        compiler_params=params(12),
        cost_estimate=busy(12),
        name="decode",
    )(limits, *queries.values(), bundle, cache, prompt_queries)
    return outs[:devices], outs[devices]


def decode_join(parts, queries, entries, local_heads):
    devices = len(parts)
    rows = entries.shape[1]
    factor = HEAD_DIM ** (-0.5) * float(np.log2(np.e))
    part_rows = rows * local_heads
    stat_rows = round_up(local_heads, 8)

    def body(*refs):
        p_refs = refs[:devices]
        q_ref, e_ref, o_ref, q_all, out = refs[devices:]
        for h in range(local_heads):
            q_all[pl.ds(h, rows, stride=local_heads), :] = q_ref[h * rows : (h + 1) * rows, :].astype(F32)
        stats = []
        for p in p_refs:
            starts = [part_rows + i * stat_rows for i in range(3)]
            high, middle, low = [p[row : row + local_heads, :].astype(F32) for row in starts]
            stats.append(high + middle + low)
        keys, values = e_ref[0].astype(F32), e_ref[1].astype(F32)
        sums = [p[0:part_rows, :].astype(F32) for p in p_refs]
        for b in range(rows):
            here = slice(b * local_heads, (b + 1) * local_heads)
            own = jnp.sum(q_all[here, :] * keys[b : b + 1, :], axis=-1, keepdims=True)
            tops = [s[:, b : b + 1] for s in stats]
            top = own
            for t in tops:
                top = jnp.maximum(top, t)
            weight = jnp.exp2((own - top) * factor)
            total = weight
            summed = weight.astype(BF16).astype(F32) * values[b : b + 1, :]
            for s, t, p in zip(stats, tops, sums):
                share = jnp.exp2((t - top) * factor)
                total = total + share * s[:, rows + b : rows + b + 1]
                summed = summed + share * p[here, :]
            out[here, :] = summed / total
        for h in range(local_heads):
            o_ref[:, h * HEAD_DIM : (h + 1) * HEAD_DIM] = out[pl.ds(h, rows, stride=local_heads), :].astype(BF16)

    return pl.pallas_call(
        body,
        in_specs=[in_vmem()] * (devices + 2),
        out_specs=in_vmem(),
        scratch_shapes=[pltpu.VMEM((part_rows, HEAD_DIM), F32)] * 2,
        out_shape=jax.ShapeDtypeStruct((rows, local_heads * HEAD_DIM), BF16),
        compiler_params=params(4),
        cost_estimate=busy(1),
        name="join",
    )(*parts, queries, entries)


def product(att, w, start, stop, targets):
    for c in range(start, stop, COLUMNS):
        width = min(COLUMNS, stop - c)
        out = jnp.dot(att, w[:, c : c + width], preferred_element_type=F32).astype(BF16)
        row = 0
        for target in targets:
            target[:, c - start : c - start + width] = out[row : row + target.shape[0]]
            row += target.shape[0]


def project(atts, weight, start):
    model = weight.shape[1]
    n = len(atts)

    def body(*refs):
        att = jnp.concatenate([ref[...] for ref in refs[:n]], axis=0)
        product(att, refs[n], start, model, refs[n + 1 :])

    return pl.pallas_call(
        body,
        in_specs=[in_vmem()] * (n + 1),
        out_specs=[in_vmem()] * n,
        out_shape=[jax.ShapeDtypeStruct((att.shape[0], model - start), BF16) for att in atts],
        compiler_params=params(8),
        cost_estimate=busy(2),
        name="project",
    )(*atts, weight)


def attend(order, first, count, block, queries, pieces, joined, decoded, weight, limits, h_rows, p_rows, columns, emit):
    history, fresh, bundle = pieces
    devices = len(history) + 1
    held = list(history)
    p_pad = fresh[0].shape[0] // 2
    local_width = queries.shape[1]
    local_heads = local_width // HEAD_DIM
    model = weight.shape[1]
    h_keys, p_keys = devices * h_rows, devices * p_pad
    keys = h_keys + p_keys
    pieces_given = joined is None
    shares = [sum(count for s in order if s % 2 == parity) for parity in (0, 1)]
    shares = [share for share in shares if share]
    factor = HEAD_DIM ** (-0.5) * float(np.log2(np.e))
    per = max(1, min(local_heads, GROUP_ROWS // count))
    has_decode = decoded is not None
    decode_rows = decoded.shape[0] if has_decode else 0

    def join_pieces(refs, k_all, v_all):
        n = devices - 1
        cached = {1: (refs[0], 0), **{k: (ref, 0) for k, ref in zip(held, refs[1:])}}
        own = {1: (refs[0], 2 * h_rows), **{k: (ref, 0) for k, ref in zip(held, refs[1 + n :])}}
        for k in range(devices):
            for part, dst in ((0, k_all), (1, v_all)):
                for copy in range(2 - part):
                    lanes = slice(copy * HEAD_DIM, (copy + 1) * HEAD_DIM)
                    ref, row = cached[k]
                    row += part * h_rows
                    dst[k * h_rows : (k + 1) * h_rows, lanes] = ref[row : row + h_rows, :]
                    ref, row = own[k]
                    row += part * p_pad
                    dst[h_keys + k * p_pad : h_keys + (k + 1) * p_pad, lanes] = ref[row : row + p_pad, :]
        v_all[:, HEAD_DIM:] = jnp.ones((keys, HEAD_DIM), BF16)

    def body(limits_ref, q, w, *refs):
        if has_decode:
            dec_ref, refs = refs[0], refs[1:]
        if pieces_given:
            parts, refs = refs[: 2 * devices - 1], refs[2 * devices - 1 :]
            k_all, v_all, refs = refs[0], refs[1], refs[2:]
            join_pieces(parts, k_all, v_all)
        else:
            k_all, v_all, refs = refs[0], refs[1], refs[2:]
        targets, att = refs[:-1], refs[-1]
        me = lax.axis_index("tp")
        column = lax.broadcasted_iota(jnp.int32, (1, h_keys), 1)
        place = ((column // h_rows) ^ me) * h_rows + column % h_rows
        history_bias = jnp.where(place < limits_ref[0:1, 0:1], 0.0, MASKED)
        column = lax.broadcasted_iota(jnp.int32, (1, p_keys), 1)
        inner = column % p_pad
        seen_from = jnp.where(inner < p_rows, ((column // p_pad) ^ me) * p_rows + inner, 1 << 20)
        steps = [(i, g) for i in range(len(order)) for g in range(0, local_heads, per)]
        biases = []
        for i, slot in enumerate(order):
            rows = (slot ^ me) * block + first + lax.broadcasted_iota(jnp.int32, (count, 1), 0)
            bias = jnp.where(seen_from <= rows, 0.0, MASKED)
            biases.append(jnp.concatenate([jnp.broadcast_to(history_bias, (count, h_keys)), bias], axis=1))

        def scores_of(i, g):
            row0 = pl.multiple_of((order[i] ^ me) * block + first, 16)
            stacked = jnp.concatenate(
                [q[pl.ds(row0, count), h * HEAD_DIM : (h + 1) * HEAD_DIM] for h in range(g, g + per)], axis=0
            )
            scaled = stacked.astype(F32) * factor
            high = scaled.astype(BF16)
            low = (scaled - high.astype(F32)).astype(BF16)
            stacked = jnp.concatenate([high, low], axis=1)
            scores = lax.dot_general(
                stacked, k_all[...], (((1,), (1,)), ((), ())), preferred_element_type=F32
            )
            return (scores.reshape(per, count, keys) + biases[i][None]).reshape(per * count, keys)

        ahead = scores_of(*steps[0])
        for t, (i, g) in enumerate(steps):
            scores = ahead
            if t + 1 < len(steps):
                ahead = scores_of(*steps[t + 1])
            top = jnp.max(scores, axis=-1, keepdims=True)
            weights = jnp.exp2(scores - top)
            summed = jnp.dot(weights.astype(BF16), v_all[...], preferred_element_type=F32)
            summed = (summed[:, :HEAD_DIM] / summed[:, HEAD_DIM:]).astype(BF16)
            for h in range(per):
                att[i * count : (i + 1) * count, (g + h) * HEAD_DIM : (g + h + 1) * HEAD_DIM] = summed[
                    h * count : (h + 1) * count
                ]
        if has_decode:
            for i, slot in enumerate(order):

                @pl.when(slot ^ me == devices - 1)
                def _():
                    att[(i + 1) * count - decode_rows : (i + 1) * count, :] = dec_ref[...]

        product(att[...], w, 0, columns, targets)

    flops = 2 * len(order) * count * (2 * local_width * keys + local_width * model)
    operands = [limits, queries, weight] + ([decoded] if has_decode else [])
    out_shape = [jax.ShapeDtypeStruct((share, columns), BF16) for share in shares]
    if pieces_given:
        operands += [bundle, *history.values(), *fresh.values()]
        out_shape = [jax.ShapeDtypeStruct((keys, 2 * HEAD_DIM), BF16)] * 2 + out_shape
    else:
        operands += joined
    attended = (len(order) * count, local_width)
    if emit:
        out_shape.append(jax.ShapeDtypeStruct(attended, BF16))
    outs = pl.pallas_call(
        body,
        in_specs=[in_vmem()] * len(operands),
        out_specs=[in_vmem()] * len(out_shape),
        out_shape=out_shape,
        scratch_shapes=[] if emit else [pltpu.VMEM(attended, BF16)],
        compiler_params=params(24),
        cost_estimate=pl.CostEstimate(flops=flops, transcendentals=0, bytes_accessed=weight.size * 2),
    )(*operands)
    if pieces_given:
        joined, outs = list(outs[:2]), outs[2:]
    return outs, joined


def finish(first, begin, residual, own, given, crossed, gain, previous):
    block, model = residual.shape
    count = crossed[0].shape[0]
    tile = 16
    n_cross = len(crossed)
    n_columns = 1 if crossed[0].shape[1] == model else 2

    def body(res_ref, own_ref, given_ref, *refs):
        cross = refs[:n_cross]
        gain_ref = refs[n_cross]
        outs = refs[-5:-3]
        staged, sem = refs[-3:-1], refs[-1]
        copies = []
        for i in range(0, count, tile):
            here, local = slice(first + i, first + i + tile), slice(i, i + tile)
            mine = slice(begin + i, begin + i + tile)
            hidden = res_ref[here, :].astype(F32) + own_ref[mine, :].astype(F32) + given_ref[mine, :].astype(F32)
            for c in range(0, n_cross, n_columns):
                pieces = [piece[local, :].astype(F32) for piece in cross[c : c + n_columns]]
                hidden = hidden + (jnp.concatenate(pieces, axis=1) if n_columns > 1 else pieces[0])
            mean = jnp.mean(hidden * hidden, axis=-1, keepdims=True)
            staged[0][local, :] = hidden.astype(BF16)
            staged[1][local, :] = (hidden * lax.rsqrt(mean + EPS) * gain_ref[...]).astype(BF16)
            for source, target in zip(staged, outs):
                copies.append(pltpu.make_async_copy(source.at[local, :], target.at[here, :], sem.at[len(copies)]))
                copies[-1].start()
        for copy in copies:
            copy.wait()

    n_in = 3 + n_cross + 1
    return pl.pallas_call(
        body,
        in_specs=[in_vmem()] * n_in + [hbm()] * len(previous),
        out_specs=[hbm()] * 2,
        out_shape=[jax.ShapeDtypeStruct((block, model), BF16)] * 2,
        input_output_aliases={n_in + i: i for i in range(len(previous))},
        scratch_shapes=[pltpu.VMEM((count, model), BF16)] * 2 + [pltpu.SemaphoreType.DMA((2 * count // tile,))],
        compiler_params=params(8),
        cost_estimate=busy(2),
    )(residual, own, given, *crossed, gain, *previous)


def step(
    prompt_queries,
    prompt_entries,
    history_cache,
    decode_queries,
    decode_entries,
    decode_cache,
    decode_lengths,
    prompt_start,
    out_weight,
    residual,
    norm_gain,
):
    devices = lax.axis_size("tp")
    local_heads = prompt_queries.shape[1] // HEAD_DIM
    kv_heads = history_cache.shape[2] // HEAD_DIM
    group = devices * local_heads // kv_heads
    block = residual.shape[0]
    h_rows, p_rows = history_cache.shape[1], prompt_entries.shape[1]
    assert group % local_heads == 0 and devices & (devices - 1) == 0
    assert block >= decode_queries.shape[0]

    def swap(value, k):
        return lax.ppermute(value, "tp", [(i, i ^ k) for i in range(devices)])

    def swapped(values):
        return [values[0]] + [swap(values[k], k) for k in range(1, devices)]

    slots = [0] + list(range(2, devices))
    packed, own_query, entries = pack_history(
        history_cache, decode_queries, decode_entries, [1] + slots, local_heads, group
    )
    rows_of = {0: own_query}
    for k in range(2, devices, 2):
        rows_of[k] = swap(own_query, k)
        rows_of[k + 1] = swap(rows_of[k], 1)
    history = {k: swap(packed[k], k) if k else packed[k] for k in slots}
    limits = jnp.concatenate([prompt_start, decode_lengths])
    limits = jnp.broadcast_to(limits[:, None], (limits.shape[0], HEAD_DIM))
    bundle, packed = pack_fresh(prompt_entries, packed[1], own_query, slots, local_heads, group)
    bundle = swap(bundle, 1)
    fresh = {k: swap(packed[k], k) if k else packed[k] for k in slots}
    parts, queries = decode_partials(rows_of, bundle, decode_cache, prompt_queries, limits, local_heads, group)
    parts = swapped(parts)
    decoded = decode_join(parts, own_query, entries, local_heads)

    joined = None

    def attended(order, first, count, decoded, columns, emit=False):
        nonlocal joined
        outs, joined = attend(
            order,
            first,
            count,
            block,
            queries,
            (history, fresh, bundle),
            joined,
            decoded,
            out_weight,
            limits,
            h_rows,
            p_rows,
            columns,
            emit,
        )
        return outs

    def chip_sum(keep, give):
        return keep.astype(F32) + swap(give, 1).astype(F32)

    def cross(pair, count, start, stop):
        return [
            swap(pair[k * count + start : k * count + stop].astype(BF16), 2 * k + 2)
            for k in range(devices // 2 - 1)
        ]

    chunks = [c * block // sum(CHUNKS) for c in CHUNKS]
    if any(c % 16 for c in chunks):
        chunks = [block]
    model = out_weight.shape[1]
    stays, leaves = list(range(2, devices, 2)), list(range(3, devices, 2))
    crossed, first = [], 0
    for count in chunks:
        last = first + count == block
        if last:
            keep, give = attended(stays + leaves, first, count, decoded, model)
            pair = chip_sum(keep, give)
            cut = count - 16 if count > 16 else 0
            for start, stop in [(0, cut), (cut, count)] if cut else [(0, count)]:
                crossed.append((first + start, cross(pair, count, start, stop)))
        else:
            columns = model // 8 * FIRST_EIGHTHS
            give, gone = attended(leaves, first, count, None, columns, emit=True)
            keep, kept = attended(stays, first, count, None, columns, emit=True)
            pieces = [cross(chip_sum(keep, give), count, 0, count)]
            keep, give = project([kept, gone], out_weight, columns)
            pieces.append(cross(chip_sum(keep, give), count, 0, count))
            crossed.append((first, [piece for both in zip(*pieces) for piece in both]))
        first += count
    owned, first = [], 0
    for count in chunks:
        here = decoded if first + count == block else None
        own, give = attended([0, 1], first, count, here, model)
        owned.append((first, own, swap(give, 1)))
        first += count
    gain = norm_gain[None, :]
    outs = []
    for first, pieces in crossed:
        begin, own, given = [o for o in owned if o[0] <= first][-1]
        outs = finish(first, first - begin, residual, own, given, pieces, gain, outs)
    return tuple(outs)


def solution(mesh):
    placed = (
        P("rep", "tp"),
        P("rep", "tp", None),
        P("rep", "tp", None),
        P("rep", "tp"),
        P("rep", None, None),
        P("rep", None, "tp", None),
        P("rep"),
        P("rep"),
        P("tp", None),
        P("tp", "rep"),
        P(),
    )
    return jax.shard_map(
        step,
        mesh=mesh,
        in_specs=placed,
        out_specs=(P("tp", "rep"), P("tp", "rep")),
        check_vma=False,
    )
```

profile of v0, /device:TPU:0, one launch (start us, length us, event | category | flops | bytes accessed | tf_op | source)
XLA Modules:
  0.0 67.7 jit_solution(10795390665299947347)
XLA Ops:
  0.6 1.0 %copy.17.p_ref = bf16[2,124,512]{2,1,0:T(8,128)(2,1)S(1)} copy(bf16[2,124,512]{2,0,1:T(2,128)(2,1)} %param.12) | data formatting | bytes 507904 | tf_op args[1]
  1.6 1.4 %pack_history.1 = (bf16[512,128]{1,0:T(8,128)(2,1)S(1)}, bf16[512,128]{1,0:T(8,128)(2,1)S(1)}, bf16[512,128]{1,0:T(8,128)(2,1)S(1)}, bf16[512,128]{1,0:T(8,128)(...) custom-call(bf16[2,256,512]{2,1,0:T(8,128)(2,1)} %h_hbm.1, bf16[16,1024]{1,0:T(8,128)(2,1)} %q_hbm.1, ...), custom_call_target="tpu_custom_call" | custom-call | flops 3000000000 | bytes 6000000 | tf_op jit(solution)/shard_map/pack_history/pallas_call | solution.py:83
  3.2 0.6 collective-permute-start.2
  3.7 2.6 %collective-permute-start = (bf16[128,128]{1,0:T(8,128)(2,1)S(1)}, bf16[128,128]{1,0:T(8,128)(2,1)S(1)}, u32[]{:S(2)}, u32[]{:S(2)}) collective-permute-start(bf16[128,128]{1,0:T(8,128)(2,1)S(1)} %get-tuple-element.35.q_ref.refs_0_.refs_4_), channel_id=1, source_target_pairs={{0,2},{1,3},{2,0},{3,1},{4,6},{5,7},{6,4},{7,5},{8,10},{9,11},{10,... | collective-permute-start | bytes 98312 | tf_op jit(solution)/shard_map/ppermute | solution.py:480
  6.4 1.4 %collective-permute-start.7 = (bf16[512,128]{1,0:T(8,128)(2,1)S(1)}, bf16[512,128]{1,0:T(8,128)(2,1)S(1)}, u32[]{:S(2)}, u32[]{:S(2)}) collective-permute-start(bf16[512,128]{1,0:T(8,128)(2,1)S(1)} %get-tuple-element.46), channel_id=1, source_target_pairs={{0,3},{1,2},{2,1},{3,0},{4,7},{5,6},{6,5},{7,4},{8,11},{9,10},{10,... | collective-permute-start | bytes 393224 | tf_op jit(solution)/shard_map/ppermute | solution.py:480
  7.8 0.5 collective-permute-start.8
  9.3 1.0 %collective-permute-done.1.refs_2_ = bf16[128,128]{1,0:T(8,128)(2,1)S(1)} collective-permute-done((bf16[128,128]{1,0:T(8,128)(2,1)S(1)}, bf16[128,128]{1,0:T(8,128)(2,1)S(1)}, u32[]{:S(2)}, u32[]{:S(2)}) %collective-permute-start.1) | collective-permute-done | bytes 32800 | tf_op jit(solution)/shard_map/ppermute | solution.py:480
  10.3 1.5 %collective-permute-start.9 = (bf16[256,128]{1,0:T(8,128)(2,1)S(1)}, bf16[256,128]{1,0:T(8,128)(2,1)S(1)}, u32[]{:S(2)}, u32[]{:S(2)}) collective-permute-start(bf16[256,128]{1,0:T(8,128)(2,1)S(1)} %get-tuple-element.49), channel_id=1, source_target_pairs={{0,3},{1,2},{2,1},{3,0},{4,7},{5,6},{6,5},{7,4},{8,11},{9,10},{10,... | collective-permute-start | bytes 196616 | tf_op jit(solution)/shard_map/ppermute | solution.py:480
  11.8 1.8 %decode.1 = (bf16[152,128]{1,0:T(8,128)(2,1)S(1)}, bf16[152,128]{1,0:T(8,128)(2,1)S(1)}, bf16[152,128]{1,0:T(8,128)(2,1)S(1)}, bf16[152,128]{1,0:T(8,128)(2,1)S(1)}, bf16[512,1024]{1,0:T(8,128)(2,1)S(1)}) custom-call(s32[17,128]{1,0:T(8,128)S(1)} %broadcast_in_dim.4.limits_ref, bf16[128,128]{1,0:T(8,128)(2,1)S(1)} %get-tuple-element.35.q_ref.refs_0_.refs_4_, ...), custom_call_target="tpu_custom_call" | custom-call | flops 6000000000 | bytes 12000000 | tf_op jit(solution)/shard_map/decode/pallas_call | solution.py:204
  13.7 3.1 %collective-permute-done.8.refs_5_ = bf16[256,128]{1,0:T(8,128)(2,1)S(1)} collective-permute-done((bf16[256,128]{1,0:T(8,128)(2,1)S(1)}, bf16[256,128]{1,0:T(8,128)(2,1)S(1)}, u32[]{:S(2)}, u32[]{:S(2)}) %collective-permute-start.8) | collective-permute-done | bytes 65568 | tf_op jit(solution)/shard_map/ppermute | solution.py:480
  16.8 2.0 %shard_map.122 = (bf16[1536,256]{1,0:T(8,128)(2,1)S(1)}, bf16[1536,256]{1,0:T(8,128)(2,1)S(1)}, bf16[64,1536]{1,0:T(8,128)(2,1)S(1)}, bf16[64,1024]{1,0:T(8,128)(2,1)S(1)}) custom-call(s32[17,128]{1,0:T(8,128)S(1)} %broadcast_in_dim.4.limits_ref, bf16[512,1024]{1,0:T(8,128)(2,1)S(1)} %get-tuple-element.38.q, bf16[1024,4096]{1,0:T(8,128)(2,1)S(1)} %bitcast.2, ...), custom_call_target="tpu_custom_call" | custom-call | flops 939524096 | bytes 8388608 | tf_op jit(solution)/shard_map/pallas_call | solution.py:401
  18.9 3.6 %shard_map.125 = (bf16[64,4096]{1,0:T(8,128)(2,1)S(1)}, bf16[64,4096]{1,0:T(8,128)(2,1)S(1)}) custom-call(s32[17,128]{1,0:T(8,128)S(1)} %broadcast_in_dim.4.limits_ref, bf16[512,1024]{1,0:T(8,128)(2,1)S(1)} %get-tuple-element.38.q, bf16[1024,4096]{1,0:T(8,128)(2,1)S(1)} %bitcast.2, bf16[1536,256]{1,0:T(8,128)(2,1)S(1)} %get-tuple-element.50.refs_1_.refs_0_, ...), custom_call_target="tpu_custom_call" | custom-call | flops 1879048192 | bytes 8388608 | tf_op jit(solution)/shard_map/pallas_call | solution.py:401
  22.4 1.9 %shard_map.126 = (bf16[64,1536]{1,0:T(8,128)(2,1)S(1)}, bf16[64,1024]{1,0:T(8,128)(2,1)S(1)}) custom-call(s32[17,128]{1,0:T(8,128)S(1)} %broadcast_in_dim.4.limits_ref, bf16[512,1024]{1,0:T(8,128)(2,1)S(1)} %get-tuple-element.38.q, bf16[1024,4096]{1,0:T(8,128)(2,1)S(1)} %bitcast.2, bf16[1536,256]{1,0:T(8,128)(2,1)S(1)} %get-tuple-element.50.refs_1_.refs_0_, ...), custom_call_target="tpu_custom_call" | custom-call | flops 939524096 | bytes 8388608 | tf_op jit(solution)/shard_map/pallas_call | solution.py:401
  24.3 0.6 collective-permute-start.3
  24.9 1.0 %collective-permute-start.4 = (bf16[152,128]{1,0:T(8,128)(2,1)S(1)}, bf16[152,128]{1,0:T(8,128)(2,1)S(1)}, u32[]{:S(2)}, u32[]{:S(2)}) collective-permute-start(bf16[152,128]{1,0:T(8,128)(2,1)S(1)} %get-tuple-element.41), channel_id=1, source_target_pairs={{0,2},{1,3},{2,0},{3,1},{4,6},{5,7},{6,4},{7,5},{8,10},{9,11},{10,... | collective-permute-start | bytes 116744 | tf_op jit(solution)/shard_map/ppermute | solution.py:480
  26.3 0.7 %collective-permute-start.14 = (bf16[64,4096]{1,0:T(8,128)(2,1)S(1)}, bf16[64,4096]{1,0:T(8,128)(2,1)S(1)}, u32[]{:S(2)}, u32[]{:S(2)}) collective-permute-start(bf16[64,4096]{1,0:T(8,128)(2,1)S(1)} %get-tuple-element.57), channel_id=1, source_target_pairs={{0,1},{1,0},{2,3},{3,2},{4,5},{5,4},{6,7},{7,6},{8,9},{9,8},{10,11... | collective-permute-start | bytes 1572872 | tf_op jit(solution)/shard_map/ppermute | solution.py:480
  27.1 0.9 %project.1 = (bf16[64,2560]{1,0:T(8,128)(2,1)S(1)}, bf16[64,2560]{1,0:T(8,128)(2,1)S(1)}) custom-call(bf16[64,1024]{1,0:T(8,128)(2,1)S(1)} %get-tuple-element.60.refs_0_, bf16[64,1024]{1,0:T(8,128)(2,1)S(1)} %get-tuple-element.61.refs_1_, bf16[1024,4096]{1,0:T(8,128)(2,1)S(1)} %bitcast.2), custom_call_target="tpu_custom_call" | custom-call | flops 1000000000 | bytes 2000000 | tf_op jit(solution)/shard_map/project/pallas_call | solution.py:285
  27.9 0.6 collective-permute-start.17
  28.9 0.8 %collective-permute-done.5.refs_3_ = bf16[152,128]{1,0:T(8,128)(2,1)S(1)} collective-permute-done((bf16[152,128]{1,0:T(8,128)(2,1)S(1)}, bf16[152,128]{1,0:T(8,128)(2,1)S(1)}, u32[]{:S(2)}, u32[]{:S(2)}) %collective-permute-start.5) | collective-permute-done | bytes 38944 | tf_op jit(solution)/shard_map/ppermute | solution.py:480
  29.7 1.2 %join.1.refs_0_ = bf16[16,1024]{1,0:T(8,128)(2,1)S(1)} custom-call(bf16[152,128]{1,0:T(8,128)(2,1)S(1)} %get-tuple-element.39.refs_0_, bf16[152,128]{1,0:T(8,128)(2,1)S(1)} %collective-permute-done.3.refs_1_, bf16[152,128]{1,0:T(8,128)(2,1)S(1)} %collective-permute-done.4.refs_2_, bf16[152,128]{1,0:T(8,128)(2,1)S(1)} %collective-permute-done.5.refs_3_, ...), custom_call_target="tpu_custom_call" | custom-call | flops 500000000 | bytes 1000000 | tf_op jit(solution)/shard_map/join/pallas_call | solution.py:255
  30.9 3.9 %shard_map.123 = (bf16[64,4096]{1,0:T(8,128)(2,1)S(1)}, bf16[64,4096]{1,0:T(8,128)(2,1)S(1)}) custom-call(s32[17,128]{1,0:T(8,128)S(1)} %broadcast_in_dim.4.limits_ref, bf16[512,1024]{1,0:T(8,128)(2,1)S(1)} %get-tuple-element.38.q, bf16[1024,4096]{1,0:T(8,128)(2,1)S(1)} %bitcast.2, bf16[16,1024]{1,0:T(8,128)(2,1)S(1)} %join.1.refs_0_, ...), custom_call_target="tpu_custom_call" | custom-call | flops 1879048192 | bytes 8388608 | tf_op jit(solution)/shard_map/pallas_call | solution.py:401
  35.0 3.7 %shard_map.124 = (bf16[64,4096]{1,0:T(8,128)(2,1)S(1)}, bf16[64,4096]{1,0:T(8,128)(2,1)S(1)}) custom-call(s32[17,128]{1,0:T(8,128)S(1)} %broadcast_in_dim.4.limits_ref, bf16[512,1024]{1,0:T(8,128)(2,1)S(1)} %get-tuple-element.38.q, bf16[1024,4096]{1,0:T(8,128)(2,1)S(1)} %bitcast.2, bf16[16,1024]{1,0:T(8,128)(2,1)S(1)} %join.1.refs_0_, ...), custom_call_target="tpu_custom_call" | custom-call | flops 1879048192 | bytes 8388608 | tf_op jit(solution)/shard_map/pallas_call | solution.py:401
  38.7 0.5 collective-permute-start.11
  39.3 1.1 %collective-permute-start.18 = (bf16[64,2560]{1,0:T(8,128)(2,1)S(1)}, bf16[64,2560]{1,0:T(8,128)(2,1)S(1)}, u32[]{:S(2)}, u32[]{:S(2)}) collective-permute-start(bf16[64,2560]{1,0:T(8,128)(2,1)S(1)} %add_convert_fusion.1), channel_id=1, source_target_pairs={{0,2},{1,3},{2,0},{3,1},{4,6},{5,7},{6,4},{7,5},{8,10},{9,11},{10,... | collective-permute-start | bytes 983048 | tf_op jit(solution)/shard_map/ppermute | solution.py:480
  40.9 1.1 %collective-permute-start.13 = (bf16[48,4096]{1,0:T(8,128)(2,1)S(1)}, bf16[48,4096]{1,0:T(8,128)(2,1)S(1)}, u32[]{:S(2)}, u32[]{:S(2)}) collective-permute-start(bf16[48,4096]{1,0:T(8,128)(2,1)S(1)} %slice.11), channel_id=1, source_target_pairs={{0,2},{1,3},{2,0},{3,1},{4,6},{5,7},{6,4},{7,5},{8,10},{9,11},{10,... | collective-permute-start | bytes 1179656 | tf_op jit(solution)/shard_map/ppermute | solution.py:480
  42.1 1.0 %collective-permute-start.16 = (bf16[64,1536]{1,0:T(8,128)(2,1)S(1)}, bf16[64,1536]{1,0:T(8,128)(2,1)S(1)}, u32[]{:S(2)}, u32[]{:S(2)}) collective-permute-start(bf16[64,1536]{1,0:T(8,128)(2,1)S(1)} %add_convert_fusion.2), channel_id=1, source_target_pairs={{0,2},{1,3},{2,0},{3,1},{4,6},{5,7},{6,4},{7,5},{8,10},{9,11},{10,... | collective-permute-start | bytes 589832 | tf_op jit(solution)/shard_map/ppermute | solution.py:480
  43.1 18.6 %collective-permute-done.16.refs_0_ = bf16[64,1536]{1,0:T(8,128)(2,1)S(1)} collective-permute-done((bf16[64,1536]{1,0:T(8,128)(2,1)S(1)}, bf16[64,1536]{1,0:T(8,128)(2,1)S(1)}, u32[]{:S(2)}, u32[]{:S(2)}) %collective-permute-start.16) | collective-permute-done | bytes 196640 | tf_op jit(solution)/shard_map/ppermute | solution.py:480
  61.7 1.0 %collective-permute-start.12 = (bf16[16,4096]{1,0:T(8,128)(2,1)S(1)}, bf16[16,4096]{1,0:T(8,128)(2,1)S(1)}, u32[]{:S(2)}, u32[]{:S(2)}) collective-permute-start(bf16[16,4096]{1,0:T(8,128)(2,1)S(1)} %slice.10), channel_id=1, source_target_pairs={{0,2},{1,3},{2,0},{3,1},{4,6},{5,7},{6,4},{7,5},{8,10},{9,11},{10,... | collective-permute-start | bytes 393224 | tf_op jit(solution)/shard_map/ppermute | solution.py:480
  62.8 1.4 %shard_map.127 = (bf16[128,4096]{1,0:T(8,128)(2,1)}, bf16[128,4096]{1,0:T(8,128)(2,1)}) custom-call(bf16[128,4096]{1,0:T(8,128)(2,1)S(1)} %copy-done, bf16[64,4096]{1,0:T(8,128)(2,1)S(1)} %get-tuple-element.56.own_ref, bf16[64,4096]{1,0:T(8,128)(2,1)S(1)} %collective-permute-done.14.given_ref, bf16[64,1536]{1,0:T(8,128)(2,1)S(1)} %collective-permute-done.16.refs_0_, ...), custom_call_target="tpu_custom_call" | custom-call | flops 1000000000 | bytes 2000000 | tf_op jit(solution)/shard_map/pallas_call | solution.py:445
  64.2 1.2 %shard_map.128 = (bf16[128,4096]{1,0:T(8,128)(2,1)}, bf16[128,4096]{1,0:T(8,128)(2,1)}) custom-call(bf16[128,4096]{1,0:T(8,128)(2,1)S(1)} %copy-done, bf16[64,4096]{1,0:T(8,128)(2,1)S(1)} %get-tuple-element.52.own_ref, bf16[64,4096]{1,0:T(8,128)(2,1)S(1)} %collective-permute-done.10.given_ref, ...), custom_call_target="tpu_custom_call", output_to_operand_aliasing={{0}: (5, {}), {1}: (6, {})} | custom-call | flops 1000000000 | bytes 2000000 | tf_op jit(solution)/shard_map/pallas_call | solution.py:445
  65.4 1.3 %collective-permute-done.12.refs_0_ = bf16[16,4096]{1,0:T(8,128)(2,1)S(1)} collective-permute-done((bf16[16,4096]{1,0:T(8,128)(2,1)S(1)}, bf16[16,4096]{1,0:T(8,128)(2,1)S(1)}, u32[]{:S(2)}, u32[]{:S(2)}) %collective-permute-start.12) | collective-permute-done | bytes 131104 | tf_op jit(solution)/shard_map/ppermute | solution.py:480
  66.7 0.9 %shard_map.129 = (bf16[128,4096]{1,0:T(8,128)(2,1)}, bf16[128,4096]{1,0:T(8,128)(2,1)}) custom-call(bf16[128,4096]{1,0:T(8,128)(2,1)S(1)} %copy-done, bf16[64,4096]{1,0:T(8,128)(2,1)S(1)} %get-tuple-element.52.own_ref, bf16[64,4096]{1,0:T(8,128)(2,1)S(1)} %collective-permute-done.10.given_ref, ...), custom_call_target="tpu_custom_call", output_to_operand_aliasing={{0}: (5, {}), {1}: (6, {})} | custom-call | flops 1000000000 | bytes 2000000 | tf_op jit(solution)/shard_map/pallas_call | solution.py:445
  (45 shorter events, 2.2 us)
Async XLA Ops:
  1.6 10.2 %slice-start.2 = ((s8[6291456]{0:T(1024)(128)(4,1)}), s8[4194304]{0:T(1024)(128)(4,1)S(1)}, s32[]{:S(2)}) async-start(s8[6291456]{0:T(1024)(128)(4,1)} %bitcast.6), calls=%async_computation.2 | async-start | bytes 8388608
  3.1 6.1 %copy-start.3 = (s32[16]{0:T(128)S(1)}, s32[16]{0:T(128)}, u32[]{:S(2)}) copy-start(s32[16]{0:T(128)} %param.17) | copy-start | bytes 196
  3.1 8.8 %slice-start.3 = ((s8[6291456]{0:T(1024)(128)(4,1)}), s8[2097152]{0:T(1024)(128)(4,1)S(1)}, s32[]{:S(2)}) async-start(s8[6291456]{0:T(1024)(128)(4,1)} %bitcast.6), calls=%async_computation.3 | async-start | bytes 4194304
  3.1 8.8 %copy-start.2 = (bf16[496,1024]{1,0:T(8,128)(2,1)S(1)}, bf16[496,1024]{1,0:T(8,128)(2,1)}, u32[]{:S(2)}) copy-start(bf16[496,1024]{1,0:T(8,128)(2,1)} %refs_5_.1) | copy-start | bytes 3047428
  3.1 13.7 %slice-start = ((s8[8388608]{0:T(1024)(128)(4,1)}), s8[4194304]{0:T(1024)(128)(4,1)S(1)}, s32[]{:S(2)}) async-start(s8[8388608]{0:T(1024)(128)(4,1)} %bitcast.1), calls=%async_computation | async-start | bytes 8388608
  3.2 8.6 %collective-permute-start.2 = (bf16[896,128]{1,0:T(8,128)(2,1)S(1)}, bf16[896,128]{1,0:T(8,128)(2,1)S(1)}, u32[]{:S(2)}, u32[]{:S(2)}) collective-permute-start(bf16[896,128]{1,0:T(8,128)(2,1)S(1)} %get-tuple-element.37), channel_id=1, source_target_pairs={{0,1},{1,0},{2,3},{3,2},{4,5},{5,4},{6,7},{7,6},{8,9},{9,8},{10,11... | collective-permute-start | bytes 688136 | tf_op jit(solution)/shard_map/ppermute | solution.py:480
  3.7 5.3 %collective-permute-start = (bf16[128,128]{1,0:T(8,128)(2,1)S(1)}, bf16[128,128]{1,0:T(8,128)(2,1)S(1)}, u32[]{:S(2)}, u32[]{:S(2)}) collective-permute-start(bf16[128,128]{1,0:T(8,128)(2,1)S(1)} %get-tuple-element.35.q_ref.refs_0_.refs_4_), channel_id=1, source_target_pairs={{0,2},{1,3},{2,0},{3,1},{4,6},{5,7},{6,4},{7,5},{8,10},{9,11},{10,... | collective-permute-start | bytes 98312 | tf_op jit(solution)/shard_map/ppermute | solution.py:480
  6.3 10.5 %collective-permute-start.6 = (bf16[512,128]{1,0:T(8,128)(2,1)S(1)}, bf16[512,128]{1,0:T(8,128)(2,1)S(1)}, u32[]{:S(2)}, u32[]{:S(2)}) collective-permute-start(bf16[512,128]{1,0:T(8,128)(2,1)S(1)} %get-tuple-element.45), channel_id=1, source_target_pairs={{0,2},{1,3},{2,0},{3,1},{4,6},{5,7},{6,4},{7,5},{8,10},{9,11},{10,... | collective-permute-start | bytes 393224 | tf_op jit(solution)/shard_map/ppermute | solution.py:480
  6.4 10.4 %collective-permute-start.7 = (bf16[512,128]{1,0:T(8,128)(2,1)S(1)}, bf16[512,128]{1,0:T(8,128)(2,1)S(1)}, u32[]{:S(2)}, u32[]{:S(2)}) collective-permute-start(bf16[512,128]{1,0:T(8,128)(2,1)S(1)} %get-tuple-element.46), channel_id=1, source_target_pairs={{0,3},{1,2},{2,1},{3,0},{4,7},{5,6},{6,5},{7,4},{8,11},{9,10},{10,... | collective-permute-start | bytes 393224 | tf_op jit(solution)/shard_map/ppermute | solution.py:480
  7.8 9.0 %collective-permute-start.8 = (bf16[256,128]{1,0:T(8,128)(2,1)S(1)}, bf16[256,128]{1,0:T(8,128)(2,1)S(1)}, u32[]{:S(2)}, u32[]{:S(2)}) collective-permute-start(bf16[256,128]{1,0:T(8,128)(2,1)S(1)} %get-tuple-element.48), channel_id=1, source_target_pairs={{0,2},{1,3},{2,0},{3,1},{4,6},{5,7},{6,4},{7,5},{8,10},{9,11},{10,... | collective-permute-start | bytes 196616 | tf_op jit(solution)/shard_map/ppermute | solution.py:480
  9.0 1.3 %collective-permute-start.1 = (bf16[128,128]{1,0:T(8,128)(2,1)S(1)}, bf16[128,128]{1,0:T(8,128)(2,1)S(1)}, u32[]{:S(2)}, u32[]{:S(2)}) collective-permute-start(bf16[128,128]{1,0:T(8,128)(2,1)S(1)} %collective-permute-done.refs_1_), channel_id=1, source_target_pairs={{0,1},{1,0},{2,3},{3,2},{4,5},{5,4},{6,7},{7,6},{8,9},{9,8},{10,11... | collective-permute-start | bytes 98312 | tf_op jit(solution)/shard_map/ppermute | solution.py:480
  10.3 6.5 %slice-start.1 = ((s8[8388608]{0:T(1024)(128)(4,1)}), s8[4194304]{0:T(1024)(128)(4,1)S(1)}, s32[]{:S(2)}) async-start(s8[8388608]{0:T(1024)(128)(4,1)} %bitcast.1), calls=%async_computation.1 | async-start | bytes 8388608
  10.3 6.5 %collective-permute-start.9 = (bf16[256,128]{1,0:T(8,128)(2,1)S(1)}, bf16[256,128]{1,0:T(8,128)(2,1)S(1)}, u32[]{:S(2)}, u32[]{:S(2)}) collective-permute-start(bf16[256,128]{1,0:T(8,128)(2,1)S(1)} %get-tuple-element.49), channel_id=1, source_target_pairs={{0,3},{1,2},{2,1},{3,0},{4,7},{5,6},{6,5},{7,4},{8,11},{9,10},{10,... | collective-permute-start | bytes 196616 | tf_op jit(solution)/shard_map/ppermute | solution.py:480
  24.3 3.6 %collective-permute-start.3 = (bf16[152,128]{1,0:T(8,128)(2,1)S(1)}, bf16[152,128]{1,0:T(8,128)(2,1)S(1)}, u32[]{:S(2)}, u32[]{:S(2)}) collective-permute-start(bf16[152,128]{1,0:T(8,128)(2,1)S(1)} %get-tuple-element.40), channel_id=1, source_target_pairs={{0,1},{1,0},{2,3},{3,2},{4,5},{5,4},{6,7},{7,6},{8,9},{9,8},{10,11... | collective-permute-start | bytes 116744 | tf_op jit(solution)/shard_map/ppermute | solution.py:480
  24.9 4.0 %collective-permute-start.4 = (bf16[152,128]{1,0:T(8,128)(2,1)S(1)}, bf16[152,128]{1,0:T(8,128)(2,1)S(1)}, u32[]{:S(2)}, u32[]{:S(2)}) collective-permute-start(bf16[152,128]{1,0:T(8,128)(2,1)S(1)} %get-tuple-element.41), channel_id=1, source_target_pairs={{0,2},{1,3},{2,0},{3,1},{4,6},{5,7},{6,4},{7,5},{8,10},{9,11},{10,... | collective-permute-start | bytes 116744 | tf_op jit(solution)/shard_map/ppermute | solution.py:480
  25.9 3.8 %collective-permute-start.5 = (bf16[152,128]{1,0:T(8,128)(2,1)S(1)}, bf16[152,128]{1,0:T(8,128)(2,1)S(1)}, u32[]{:S(2)}, u32[]{:S(2)}) collective-permute-start(bf16[152,128]{1,0:T(8,128)(2,1)S(1)} %get-tuple-element.42), channel_id=1, source_target_pairs={{0,3},{1,2},{2,1},{3,0},{4,7},{5,6},{6,5},{7,4},{8,11},{9,10},{10,... | collective-permute-start | bytes 116744 | tf_op jit(solution)/shard_map/ppermute | solution.py:480
  26.3 36.4 %collective-permute-start.14 = (bf16[64,4096]{1,0:T(8,128)(2,1)S(1)}, bf16[64,4096]{1,0:T(8,128)(2,1)S(1)}, u32[]{:S(2)}, u32[]{:S(2)}) collective-permute-start(bf16[64,4096]{1,0:T(8,128)(2,1)S(1)} %get-tuple-element.57), channel_id=1, source_target_pairs={{0,1},{1,0},{2,3},{3,2},{4,5},{5,4},{6,7},{7,6},{8,9},{9,8},{10,11... | collective-permute-start | bytes 1572872 | tf_op jit(solution)/shard_map/ppermute | solution.py:480
  27.1 15.0 %collective-permute-start.15 = (bf16[64,1536]{1,0:T(8,128)(2,1)S(1)}, bf16[64,1536]{1,0:T(8,128)(2,1)S(1)}, u32[]{:S(2)}, u32[]{:S(2)}) collective-permute-start(bf16[64,1536]{1,0:T(8,128)(2,1)S(1)} %get-tuple-element.59), channel_id=1, source_target_pairs={{0,1},{1,0},{2,3},{3,2},{4,5},{5,4},{6,7},{7,6},{8,9},{9,8},{10,11... | collective-permute-start | bytes 589832 | tf_op jit(solution)/shard_map/ppermute | solution.py:480
  27.9 11.3 %collective-permute-start.17 = (bf16[64,2560]{1,0:T(8,128)(2,1)S(1)}, bf16[64,2560]{1,0:T(8,128)(2,1)S(1)}, u32[]{:S(2)}, u32[]{:S(2)}) collective-permute-start(bf16[64,2560]{1,0:T(8,128)(2,1)S(1)} %get-tuple-element.63), channel_id=1, source_target_pairs={{0,1},{1,0},{2,3},{3,2},{4,5},{5,4},{6,7},{7,6},{8,9},{9,8},{10,11... | collective-permute-start | bytes 983048 | tf_op jit(solution)/shard_map/ppermute | solution.py:480
  34.8 28.0 %copy-start = (bf16[128,4096]{1,0:T(8,128)(2,1)S(1)}, bf16[128,4096]{1,0:T(8,128)(2,1)}, u32[]{:S(2)}) copy-start(bf16[128,4096]{1,0:T(8,128)(2,1)} %res_ref.5) | copy-start | bytes 3145732
  34.8 28.0 %copy-start.1 = (f32[4096]{0:T(1024)S(1)}, f32[4096]{0:T(1024)}, u32[]{:S(2)}) copy-start(f32[4096]{0:T(1024)} %param.21) | copy-start | bytes 49156
  34.8 29.3 %collective-permute-start.10 = (bf16[64,4096]{1,0:T(8,128)(2,1)S(1)}, bf16[64,4096]{1,0:T(8,128)(2,1)S(1)}, u32[]{:S(2)}, u32[]{:S(2)}) collective-permute-start(bf16[64,4096]{1,0:T(8,128)(2,1)S(1)} %get-tuple-element.53), channel_id=1, source_target_pairs={{0,1},{1,0},{2,3},{3,2},{4,5},{5,4},{6,7},{7,6},{8,9},{9,8},{10,11... | collective-permute-start | bytes 1572872 | tf_op jit(solution)/shard_map/ppermute | solution.py:480
  38.7 2.0 %collective-permute-start.11 = (bf16[64,4096]{1,0:T(8,128)(2,1)S(1)}, bf16[64,4096]{1,0:T(8,128)(2,1)S(1)}, u32[]{:S(2)}, u32[]{:S(2)}) collective-permute-start(bf16[64,4096]{1,0:T(8,128)(2,1)S(1)} %get-tuple-element.55), channel_id=1, source_target_pairs={{0,1},{1,0},{2,3},{3,2},{4,5},{5,4},{6,7},{7,6},{8,9},{9,8},{10,11... | collective-permute-start | bytes 1572872 | tf_op jit(solution)/shard_map/ppermute | solution.py:480
  39.3 23.5 %collective-permute-start.18 = (bf16[64,2560]{1,0:T(8,128)(2,1)S(1)}, bf16[64,2560]{1,0:T(8,128)(2,1)S(1)}, u32[]{:S(2)}, u32[]{:S(2)}) collective-permute-start(bf16[64,2560]{1,0:T(8,128)(2,1)S(1)} %add_convert_fusion.1), channel_id=1, source_target_pairs={{0,2},{1,3},{2,0},{3,1},{4,6},{5,7},{6,4},{7,5},{8,10},{9,11},{10,... | collective-permute-start | bytes 983048 | tf_op jit(solution)/shard_map/ppermute | solution.py:480
  40.9 23.3 %collective-permute-start.13 = (bf16[48,4096]{1,0:T(8,128)(2,1)S(1)}, bf16[48,4096]{1,0:T(8,128)(2,1)S(1)}, u32[]{:S(2)}, u32[]{:S(2)}) collective-permute-start(bf16[48,4096]{1,0:T(8,128)(2,1)S(1)} %slice.11), channel_id=1, source_target_pairs={{0,2},{1,3},{2,0},{3,1},{4,6},{5,7},{6,4},{7,5},{8,10},{9,11},{10,... | collective-permute-start | bytes 1179656 | tf_op jit(solution)/shard_map/ppermute | solution.py:480
  42.1 19.6 %collective-permute-start.16 = (bf16[64,1536]{1,0:T(8,128)(2,1)S(1)}, bf16[64,1536]{1,0:T(8,128)(2,1)S(1)}, u32[]{:S(2)}, u32[]{:S(2)}) collective-permute-start(bf16[64,1536]{1,0:T(8,128)(2,1)S(1)} %add_convert_fusion.2), channel_id=1, source_target_pairs={{0,2},{1,3},{2,0},{3,1},{4,6},{5,7},{6,4},{7,5},{8,10},{9,11},{10,... | collective-permute-start | bytes 589832 | tf_op jit(solution)/shard_map/ppermute | solution.py:480
  61.7 5.0 %collective-permute-start.12 = (bf16[16,4096]{1,0:T(8,128)(2,1)S(1)}, bf16[16,4096]{1,0:T(8,128)(2,1)S(1)}, u32[]{:S(2)}, u32[]{:S(2)}) collective-permute-start(bf16[16,4096]{1,0:T(8,128)(2,1)S(1)} %slice.10), channel_id=1, source_target_pairs={{0,2},{1,3},{2,0},{3,1},{4,6},{5,7},{6,4},{7,5},{8,10},{9,11},{10,... | collective-permute-start | bytes 393224 | tf_op jit(solution)/shard_map/ppermute | solution.py:480
where the time goes:
time: 67.9 us; the launch traced here: 67.7 us
  waiting for transfers between devices  25.6 us (38%)
  Pallas kernels  23.9 us (35%)
  starting transfers between devices  15 us (22%)
  between operations  1.71 us (3%)
  local copies, waits for them, and re-layouts  1.13 us (2%)
    ppermute x19, waiting for transfers between devices, swap(): return lax.ppermute(value, 'tp', [(i, i ^ k) for i in range(devices)])  25.6 us
    pallas_call x5, Pallas kernels, attend(): pl.pallas_call(body, in_specs=[in_vmem()] * len(operands), out_specs=[in_...  15.1 us
    ppermute x19, starting transfers between devices, swap(): return lax.ppermute(value, 'tp', [(i, i ^ k) for i in range(devices)])  15 us
    pallas_call x3, Pallas kernels, finish(): pl.pallas_call(body, in_specs=[in_vmem()] * n_in + [hbm()] * len(previous...  3.45 us
    pallas_call x1, Pallas kernels, decode_partials(): pl.pallas_call(body, in_specs=[in_vmem()] * (devices + 3), out_specs=[in_...  1.8 us
    pallas_call x1, Pallas kernels, pack_history(): pl.pallas_call(body, in_specs=[in_hbm()] * 3, out_specs=[in_vmem()] * (de...  1.42 us
  transfers between devices with their start and end apart: 19, of which 7 were waited for; matrix products, arithmetic and copies ran while one was open for 1% of the time, Pallas kernels for 21%

commit v1 on v0

--- a/solution.py
+++ b/solution.py
@@ -97,13 +97,15 @@
     return dict(zip(slots, outs)), outs[devices], outs[devices + 1]
 
 
-def pack_fresh(prompt, history, query, slots, local_heads, group):
+def pack_fresh(prompt, history, queries, slots, local_heads, group):
     h_rows, p_rows = history.shape[0] // 2, prompt.shape[1]
     p_pad = round_up(p_rows, 16)
+    q_rows = queries[0].shape[0]
     every = [1] + slots
     n = len(every)
 
-    def body(p_ref, h_ref, q_ref, *o_refs):
+    def body(p_ref, h_ref, *refs):
+        q_refs, o_refs = refs[: len(queries)], refs[len(queries) :]
         me = lax.axis_index("tp")
         o_refs[0][0 : 2 * h_rows, :] = h_ref[...]
         for i, k in enumerate(every):
@@ -116,18 +118,20 @@
                         [fresh.astype(F32), jnp.zeros((p_pad - p_rows, HEAD_DIM), F32)], axis=0
                     ).astype(BF16)
                 o_refs[i][row + part * p_pad : row + (part + 1) * p_pad, :] = fresh
-        o_refs[0][2 * (h_rows + p_pad) :, :] = q_ref[...]
-
-    sizes = [2 * (h_rows + p_pad) + query.shape[0]] + [2 * p_pad] * len(slots)
+        row = 2 * (h_rows + p_pad)
+        for i, q_ref in enumerate(q_refs):
+            o_refs[0][row + i * q_rows : row + (i + 1) * q_rows, :] = q_ref[...]
+
+    sizes = [2 * (h_rows + p_pad) + len(queries) * q_rows] + [2 * p_pad] * len(slots)
     outs = pl.pallas_call(
         body,
-        in_specs=[in_vmem()] * 3,
+        in_specs=[in_vmem()] * (2 + len(queries)),
         out_specs=[in_vmem()] * n,
         out_shape=[jax.ShapeDtypeStruct((size, HEAD_DIM), BF16) for size in sizes],
         compiler_params=params(8),
         cost_estimate=busy(12),
         name="pack_fresh",
-    )(prompt, history, query)
+    )(prompt, history, *queries)
     return outs[0], dict(zip(slots, outs[1:]))
 
 
@@ -140,8 +144,7 @@
 
 
 def decode_partials(queries, bundle, cache, prompt_queries, limits, local_heads, group):
-    devices = len(queries) + 1
-    held = list(queries)
+    devices = 2 * len(queries)
     rows, span, width = cache.shape[1], cache.shape[2], cache.shape[3]
     kv_heads = width // HEAD_DIM
     heads = devices * local_heads
@@ -151,7 +154,7 @@
     prompt_rows, local_width = prompt_queries.shape
 
     def body(limits_ref, *refs):
-        q_refs, refs = dict(zip(held, refs)), refs[devices - 1 :]
+        q_refs, refs = refs[: devices // 2], refs[devices // 2 :]
         bundle_ref, cache_ref, pq_ref = refs[:3]
         o_refs, refs = refs[3 : 3 + devices], refs[3 + devices :]
         q_ref, q_all, sums = refs
@@ -159,7 +162,8 @@
         q_ref[0:prompt_rows, :] = pq_ref[...]
         q_ref[prompt_rows:, :] = jnp.zeros((rows, local_width), BF16)
         for k in range(devices):
-            q_ref_k, base = (bundle_ref, bundle.shape[0] - part_rows) if k == 1 else (q_refs[k], 0)
+            base = bundle.shape[0] - (devices // 2 - k // 2) * part_rows if k % 2 else 0
+            q_ref_k = bundle_ref if k % 2 else q_refs[k // 2]
             for h in range(local_heads):
                 row = base + h * rows
                 q_all[k, pl.ds(h, rows, stride=local_heads), :] = q_ref_k[row : row + rows, :].astype(F32)
@@ -203,7 +207,7 @@
 
     outs = pl.pallas_call(
         body,
-        in_specs=[in_vmem()] * (devices + 3),
+        in_specs=[in_vmem()] * (devices // 2 + 4),
         out_specs=[in_vmem()] * (devices + 1),
         scratch_shapes=[pltpu.VMEM((devices, part_rows, HEAD_DIM), F32)] * 2,
         out_shape=[jax.ShapeDtypeStruct((part_rows + 3 * stat_rows, HEAD_DIM), BF16)] * devices
@@ -211,7 +215,7 @@
         compiler_params=params(12),
         cost_estimate=busy(12),
         name="decode",
-    )(limits, *queries.values(), bundle, cache, prompt_queries)
+    )(limits, *queries, bundle, cache, prompt_queries)
     return outs[:devices], outs[devices]
 
 
@@ -486,17 +490,14 @@
     packed, own_query, entries = pack_history(
         history_cache, decode_queries, decode_entries, [1] + slots, local_heads, group
     )
-    rows_of = {0: own_query}
-    for k in range(2, devices, 2):
-        rows_of[k] = swap(own_query, k)
-        rows_of[k + 1] = swap(rows_of[k], 1)
+    even_queries = [own_query] + [swap(own_query, k) for k in range(2, devices, 2)]
     history = {k: swap(packed[k], k) if k else packed[k] for k in slots}
     limits = jnp.concatenate([prompt_start, decode_lengths])
     limits = jnp.broadcast_to(limits[:, None], (limits.shape[0], HEAD_DIM))
-    bundle, packed = pack_fresh(prompt_entries, packed[1], own_query, slots, local_heads, group)
+    bundle, packed = pack_fresh(prompt_entries, packed[1], even_queries, slots, local_heads, group)
     bundle = swap(bundle, 1)
     fresh = {k: swap(packed[k], k) if k else packed[k] for k in slots}
-    parts, queries = decode_partials(rows_of, bundle, decode_cache, prompt_queries, limits, local_heads, group)
+    parts, queries = decode_partials(even_queries, bundle, decode_cache, prompt_queries, limits, local_heads, group)
     parts = swapped(parts)
     decoded = decode_join(parts, own_query, entries, local_heads)
 

time: 67.9 us -> 70 us (1.031)
  waiting for transfers between devices: 25.6 us -> 30.2 us
  starting transfers between devices: 15 us -> 13.8 us
  local copies, waits for them, and re-layouts: 1.13 us -> 0.17 us
    ppermute x19 -> x18, waiting for transfers between devices: 25.6 us -> 30.2 us  [swap(): return lax.ppermute(value, 'tp', [(i, i ^ k) for i in range(devices)])]
    ppermute x19 -> x18, starting transfers between devices: 15 us -> 13.8 us  [swap(): return lax.ppermute(value, 'tp', [(i, i ^ k) for i in range(devices)])]
    unnamed x17 -> x19, local copies, waits for them, and re-layouts: 1.03 us -> 0.07 us
  transfers between devices with their start and end apart: 19 -> 18, of which waited for: 7 -> 8; matrix products, arithmetic and copies ran while one was open for 1% -> 1% of each run, Pallas kernels for 21% -> 20%
where the time goes in v1:
time: 70 us; the launch traced here: 69.9 us
  waiting for transfers between devices  30.2 us (43%)
  Pallas kernels  23.7 us (34%)
  starting transfers between devices  13.8 us (20%)
  between operations  1.68 us (2%)
    ppermute x18, waiting for transfers between devices, swap(): return lax.ppermute(value, 'tp', [(i, i ^ k) for i in range(devices)])  30.2 us
    pallas_call x5, Pallas kernels, attend(): pl.pallas_call(body, in_specs=[in_vmem()] * len(operands), out_specs=[in_...  15.1 us
    ppermute x18, starting transfers between devices, swap(): return lax.ppermute(value, 'tp', [(i, i ^ k) for i in range(devices)])  13.8 us
    pallas_call x3, Pallas kernels, finish(): pl.pallas_call(body, in_specs=[in_vmem()] * n_in + [hbm()] * len(previous...  3.45 us
    pallas_call x1, Pallas kernels, decode_partials(): pl.pallas_call(body, in_specs=[in_vmem()] * (devices // 2 + 4), out_specs...  1.75 us
  transfers between devices with their start and end apart: 18, of which 8 were waited for; matrix products, arithmetic and copies ran while one was open for 1% of the time, Pallas kernels for 20%

profile of v1, /device:TPU:0, one launch (start us, length us, event | category | flops | bytes accessed | tf_op | source)
XLA Modules:
  0.0 69.9 jit_solution(1978835429074744334)
XLA Ops:
  0.6 1.3 %pack_history.1 = (bf16[512,128]{1,0:T(8,128)(2,1)S(1)}, bf16[512,128]{1,0:T(8,128)(2,1)S(1)}, bf16[512,128]{1,0:T(8,128)(2,1)S(1)}, bf16[512,128]{1,0:T(8,128)(...) custom-call(bf16[2,256,512]{2,1,0:T(8,128)(2,1)} %h_hbm.1, bf16[16,1024]{1,0:T(8,128)(2,1)} %q_hbm.1, ...), custom_call_target="tpu_custom_call" | custom-call | flops 3000000000 | bytes 6000000 | tf_op jit(solution)/shard_map/pack_history/pallas_call | solution.py:83
  2.0 3.1 %collective-permute-start = (bf16[128,128]{1,0:T(8,128)(2,1)S(1)}, bf16[128,128]{1,0:T(8,128)(2,1)S(1)}, u32[]{:S(2)}, u32[]{:S(2)}) collective-permute-start(bf16[128,128]{1,0:T(8,128)(2,1)S(1)} %get-tuple-element.35.refs_0_.refs_4_), channel_id=1, source_target_pairs={{0,2},{1,3},{2,0},{3,1},{4,6},{5,7},{6,4},{7,5},{8,10},{9,11},{10,... | collective-permute-start | bytes 98312 | tf_op jit(solution)/shard_map/ppermute | solution.py:484
  5.1 1.9 %collective-permute-done.refs_1_ = bf16[128,128]{1,0:T(8,128)(2,1)S(1)} collective-permute-done((bf16[128,128]{1,0:T(8,128)(2,1)S(1)}, bf16[128,128]{1,0:T(8,128)(2,1)S(1)}, u32[]{:S(2)}, u32[]{:S(2)}) %collective-permute-start) | collective-permute-done | bytes 32800 | tf_op jit(solution)/shard_map/ppermute | solution.py:484
  7.1 2.1 %collective-permute-start.5 = (bf16[512,128]{1,0:T(8,128)(2,1)S(1)}, bf16[512,128]{1,0:T(8,128)(2,1)S(1)}, u32[]{:S(2)}, u32[]{:S(2)}) collective-permute-start(bf16[512,128]{1,0:T(8,128)(2,1)S(1)} %get-tuple-element.45), channel_id=1, source_target_pairs={{0,2},{1,3},{2,0},{3,1},{4,6},{5,7},{6,4},{7,5},{8,10},{9,11},{10,... | collective-permute-start | bytes 393224 | tf_op jit(solution)/shard_map/ppermute | solution.py:484
  9.9 1.9 %collective-permute-start.7 = (bf16[256,128]{1,0:T(8,128)(2,1)S(1)}, bf16[256,128]{1,0:T(8,128)(2,1)S(1)}, u32[]{:S(2)}, u32[]{:S(2)}) collective-permute-start(bf16[256,128]{1,0:T(8,128)(2,1)S(1)} %get-tuple-element.48), channel_id=1, source_target_pairs={{0,2},{1,3},{2,0},{3,1},{4,6},{5,7},{6,4},{7,5},{8,10},{9,11},{10,... | collective-permute-start | bytes 196616 | tf_op jit(solution)/shard_map/ppermute | solution.py:484
  11.9 1.7 %decode.1 = (bf16[152,128]{1,0:T(8,128)(2,1)S(1)}, bf16[152,128]{1,0:T(8,128)(2,1)S(1)}, bf16[152,128]{1,0:T(8,128)(2,1)S(1)}, bf16[152,128]{1,0:T(8,128)(2,1)S(1)}, bf16[512,1024]{1,0:T(8,128)(2,1)S(1)}) custom-call(s32[17,128]{1,0:T(8,128)S(1)} %broadcast_in_dim.4.limits_ref, bf16[128,128]{1,0:T(8,128)(2,1)S(1)} %get-tuple-element.35.refs_0_.refs_4_, ...), custom_call_target="tpu_custom_call" | custom-call | flops 6000000000 | bytes 12000000 | tf_op jit(solution)/shard_map/decode/pallas_call | solution.py:208
  13.7 4.1 %collective-permute-done.7.refs_5_ = bf16[256,128]{1,0:T(8,128)(2,1)S(1)} collective-permute-done((bf16[256,128]{1,0:T(8,128)(2,1)S(1)}, bf16[256,128]{1,0:T(8,128)(2,1)S(1)}, u32[]{:S(2)}, u32[]{:S(2)}) %collective-permute-start.7) | collective-permute-done | bytes 65568 | tf_op jit(solution)/shard_map/ppermute | solution.py:484
  17.7 0.9 %collective-permute-done.8.refs_6_ = bf16[256,128]{1,0:T(8,128)(2,1)S(1)} collective-permute-done((bf16[256,128]{1,0:T(8,128)(2,1)S(1)}, bf16[256,128]{1,0:T(8,128)(2,1)S(1)}, u32[]{:S(2)}, u32[]{:S(2)}) %collective-permute-start.8) | collective-permute-done | bytes 65568 | tf_op jit(solution)/shard_map/ppermute | solution.py:484
  18.6 2.0 %shard_map.122 = (bf16[1536,256]{1,0:T(8,128)(2,1)S(1)}, bf16[1536,256]{1,0:T(8,128)(2,1)S(1)}, bf16[64,1536]{1,0:T(8,128)(2,1)S(1)}, bf16[64,1024]{1,0:T(8,128)(2,1)S(1)}) custom-call(s32[17,128]{1,0:T(8,128)S(1)} %broadcast_in_dim.4.limits_ref, bf16[512,1024]{1,0:T(8,128)(2,1)S(1)} %get-tuple-element.38.q, bf16[1024,4096]{1,0:T(8,128)(2,1)S(1)} %bitcast.2, ...), custom_call_target="tpu_custom_call" | custom-call | flops 939524096 | bytes 8388608 | tf_op jit(solution)/shard_map/pallas_call | solution.py:405
  20.7 3.6 %shard_map.125 = (bf16[64,4096]{1,0:T(8,128)(2,1)S(1)}, bf16[64,4096]{1,0:T(8,128)(2,1)S(1)}) custom-call(s32[17,128]{1,0:T(8,128)S(1)} %broadcast_in_dim.4.limits_ref, bf16[512,1024]{1,0:T(8,128)(2,1)S(1)} %get-tuple-element.38.q, bf16[1024,4096]{1,0:T(8,128)(2,1)S(1)} %bitcast.2, bf16[1536,256]{1,0:T(8,128)(2,1)S(1)} %get-tuple-element.50.refs_1_.refs_0_, ...), custom_call_target="tpu_custom_call" | custom-call | flops 1879048192 | bytes 8388608 | tf_op jit(solution)/shard_map/pallas_call | solution.py:405
  24.2 1.9 %shard_map.126 = (bf16[64,1536]{1,0:T(8,128)(2,1)S(1)}, bf16[64,1024]{1,0:T(8,128)(2,1)S(1)}) custom-call(s32[17,128]{1,0:T(8,128)S(1)} %broadcast_in_dim.4.limits_ref, bf16[512,1024]{1,0:T(8,128)(2,1)S(1)} %get-tuple-element.38.q, bf16[1024,4096]{1,0:T(8,128)(2,1)S(1)} %bitcast.2, bf16[1536,256]{1,0:T(8,128)(2,1)S(1)} %get-tuple-element.50.refs_1_.refs_0_, ...), custom_call_target="tpu_custom_call" | custom-call | flops 939524096 | bytes 8388608 | tf_op jit(solution)/shard_map/pallas_call | solution.py:405
  26.2 0.2 collective-permute-start.2
  26.3 1.7 %collective-permute-start.3 = (bf16[152,128]{1,0:T(8,128)(2,1)S(1)}, bf16[152,128]{1,0:T(8,128)(2,1)S(1)}, u32[]{:S(2)}, u32[]{:S(2)}) collective-permute-start(bf16[152,128]{1,0:T(8,128)(2,1)S(1)} %get-tuple-element.41), channel_id=1, source_target_pairs={{0,2},{1,3},{2,0},{3,1},{4,6},{5,7},{6,4},{7,5},{8,10},{9,11},{10,... | collective-permute-start | bytes 116744 | tf_op jit(solution)/shard_map/ppermute | solution.py:484
  28.1 0.4 collective-permute-start.13
  28.6 0.9 %project.1 = (bf16[64,2560]{1,0:T(8,128)(2,1)S(1)}, bf16[64,2560]{1,0:T(8,128)(2,1)S(1)}) custom-call(bf16[64,1024]{1,0:T(8,128)(2,1)S(1)} %get-tuple-element.60.refs_0_, bf16[64,1024]{1,0:T(8,128)(2,1)S(1)} %get-tuple-element.61.refs_1_, bf16[1024,4096]{1,0:T(8,128)(2,1)S(1)} %bitcast.2), custom_call_target="tpu_custom_call" | custom-call | flops 1000000000 | bytes 2000000 | tf_op jit(solution)/shard_map/project/pallas_call | solution.py:289
  29.5 0.5 collective-permute-start.16
  29.9 0.4 collective-permute-done.3.refs_2_
  30.3 1.5 %collective-permute-done.4.refs_3_ = bf16[152,128]{1,0:T(8,128)(2,1)S(1)} collective-permute-done((bf16[152,128]{1,0:T(8,128)(2,1)S(1)}, bf16[152,128]{1,0:T(8,128)(2,1)S(1)}, u32[]{:S(2)}, u32[]{:S(2)}) %collective-permute-start.4) | collective-permute-done | bytes 38944 | tf_op jit(solution)/shard_map/ppermute | solution.py:484
  31.8 1.2 %join.1.refs_0_ = bf16[16,1024]{1,0:T(8,128)(2,1)S(1)} custom-call(bf16[152,128]{1,0:T(8,128)(2,1)S(1)} %get-tuple-element.39.refs_0_, bf16[152,128]{1,0:T(8,128)(2,1)S(1)} %collective-permute-done.2.refs_1_, bf16[152,128]{1,0:T(8,128)(2,1)S(1)} %collective-permute-done.3.refs_2_, bf16[152,128]{1,0:T(8,128)(2,1)S(1)} %collective-permute-done.4.refs_3_, ...), custom_call_target="tpu_custom_call" | custom-call | flops 500000000 | bytes 1000000 | tf_op jit(solution)/shard_map/join/pallas_call | solution.py:259
  33.0 3.9 %shard_map.123 = (bf16[64,4096]{1,0:T(8,128)(2,1)S(1)}, bf16[64,4096]{1,0:T(8,128)(2,1)S(1)}) custom-call(s32[17,128]{1,0:T(8,128)S(1)} %broadcast_in_dim.4.limits_ref, bf16[512,1024]{1,0:T(8,128)(2,1)S(1)} %get-tuple-element.38.q, bf16[1024,4096]{1,0:T(8,128)(2,1)S(1)} %bitcast.2, bf16[16,1024]{1,0:T(8,128)(2,1)S(1)} %join.1.refs_0_, ...), custom_call_target="tpu_custom_call" | custom-call | flops 1879048192 | bytes 8388608 | tf_op jit(solution)/shard_map/pallas_call | solution.py:405
  37.1 3.7 %shard_map.124 = (bf16[64,4096]{1,0:T(8,128)(2,1)S(1)}, bf16[64,4096]{1,0:T(8,128)(2,1)S(1)}) custom-call(s32[17,128]{1,0:T(8,128)S(1)} %broadcast_in_dim.4.limits_ref, bf16[512,1024]{1,0:T(8,128)(2,1)S(1)} %get-tuple-element.38.q, bf16[1024,4096]{1,0:T(8,128)(2,1)S(1)} %bitcast.2, bf16[16,1024]{1,0:T(8,128)(2,1)S(1)} %join.1.refs_0_, ...), custom_call_target="tpu_custom_call" | custom-call | flops 1879048192 | bytes 8388608 | tf_op jit(solution)/shard_map/pallas_call | solution.py:405
  40.9 0.5 collective-permute-start.10
  41.4 0.4 collective-permute-start.17
  41.9 1.0 %collective-permute-done.10 = bf16[64,4096]{1,0:T(8,128)(2,1)S(1)} collective-permute-done((bf16[64,4096]{1,0:T(8,128)(2,1)S(1)}, bf16[64,4096]{1,0:T(8,128)(2,1)S(1)}, u32[]{:S(2)}, u32[]{:S(2)}) %collective-permute-start.10) | collective-permute-done | bytes 524320 | tf_op jit(solution)/shard_map/ppermute | solution.py:484
  43.0 0.7 %collective-permute-start.12 = (bf16[48,4096]{1,0:T(8,128)(2,1)S(1)}, bf16[48,4096]{1,0:T(8,128)(2,1)S(1)}, u32[]{:S(2)}, u32[]{:S(2)}) collective-permute-start(bf16[48,4096]{1,0:T(8,128)(2,1)S(1)} %slice.11), channel_id=1, source_target_pairs={{0,2},{1,3},{2,0},{3,1},{4,6},{5,7},{6,4},{7,5},{8,10},{9,11},{10,... | collective-permute-start | bytes 1179656 | tf_op jit(solution)/shard_map/ppermute | solution.py:484
  43.8 1.4 %collective-permute-start.15 = (bf16[64,1536]{1,0:T(8,128)(2,1)S(1)}, bf16[64,1536]{1,0:T(8,128)(2,1)S(1)}, u32[]{:S(2)}, u32[]{:S(2)}) collective-permute-start(bf16[64,1536]{1,0:T(8,128)(2,1)S(1)} %add_convert_fusion.2), channel_id=1, source_target_pairs={{0,2},{1,3},{2,0},{3,1},{4,6},{5,7},{6,4},{7,5},{8,10},{9,11},{10,... | collective-permute-start | bytes 589832 | tf_op jit(solution)/shard_map/ppermute | solution.py:484
  45.2 18.6 %collective-permute-done.15.refs_0_ = bf16[64,1536]{1,0:T(8,128)(2,1)S(1)} collective-permute-done((bf16[64,1536]{1,0:T(8,128)(2,1)S(1)}, bf16[64,1536]{1,0:T(8,128)(2,1)S(1)}, u32[]{:S(2)}, u32[]{:S(2)}) %collective-permute-start.15) | collective-permute-done | bytes 196640 | tf_op jit(solution)/shard_map/ppermute | solution.py:484
  63.8 0.5 collective-permute-start.11
  64.4 1.4 %shard_map.127 = (bf16[128,4096]{1,0:T(8,128)(2,1)}, bf16[128,4096]{1,0:T(8,128)(2,1)}) custom-call(bf16[128,4096]{1,0:T(8,128)(2,1)S(1)} %copy-done, bf16[64,4096]{1,0:T(8,128)(2,1)S(1)} %get-tuple-element.56.own_ref, bf16[64,4096]{1,0:T(8,128)(2,1)S(1)} %collective-permute-done.13.given_ref, bf16[64,1536]{1,0:T(8,128)(2,1)S(1)} %collective-permute-done.15.refs_0_, ...), custom_call_target="tpu_custom_call" | custom-call | flops 1000000000 | bytes 2000000 | tf_op jit(solution)/shard_map/pallas_call | solution.py:449
  65.8 1.2 %shard_map.128 = (bf16[128,4096]{1,0:T(8,128)(2,1)}, bf16[128,4096]{1,0:T(8,128)(2,1)}) custom-call(bf16[128,4096]{1,0:T(8,128)(2,1)S(1)} %copy-done, bf16[64,4096]{1,0:T(8,128)(2,1)S(1)} %get-tuple-element.52.own_ref, bf16[64,4096]{1,0:T(8,128)(2,1)S(1)} %collective-permute-done.9.given_ref, ...), custom_call_target="tpu_custom_call", output_to_operand_aliasing={{0}: (5, {}), {1}: (6, {})} | custom-call | flops 1000000000 | bytes 2000000 | tf_op jit(solution)/shard_map/pallas_call | solution.py:449
  67.0 1.8 %collective-permute-done.11.refs_0_ = bf16[16,4096]{1,0:T(8,128)(2,1)S(1)} collective-permute-done((bf16[16,4096]{1,0:T(8,128)(2,1)S(1)}, bf16[16,4096]{1,0:T(8,128)(2,1)S(1)}, u32[]{:S(2)}, u32[]{:S(2)}) %collective-permute-start.11) | collective-permute-done | bytes 131104 | tf_op jit(solution)/shard_map/ppermute | solution.py:484
  68.8 0.9 %shard_map.129 = (bf16[128,4096]{1,0:T(8,128)(2,1)}, bf16[128,4096]{1,0:T(8,128)(2,1)}) custom-call(bf16[128,4096]{1,0:T(8,128)(2,1)S(1)} %copy-done, bf16[64,4096]{1,0:T(8,128)(2,1)S(1)} %get-tuple-element.52.own_ref, bf16[64,4096]{1,0:T(8,128)(2,1)S(1)} %collective-permute-done.9.given_ref, ...), custom_call_target="tpu_custom_call", output_to_operand_aliasing={{0}: (5, {}), {1}: (6, {})} | custom-call | flops 1000000000 | bytes 2000000 | tf_op jit(solution)/shard_map/pallas_call | solution.py:449
  (45 shorter events, 1.0 us)
Async XLA Ops:
  0.6 4.4 %copy-start.3 = (bf16[2,124,512]{2,0,1:T(2,128)(2,1)S(1)}, bf16[2,124,512]{2,0,1:T(2,128)(2,1)}, u32[]{:S(2)}) copy-start(bf16[2,124,512]{2,0,1:T(2,128)(2,1)} %param.12) | copy-start | bytes 761860
  2.0 5.0 %collective-permute-start = (bf16[128,128]{1,0:T(8,128)(2,1)S(1)}, bf16[128,128]{1,0:T(8,128)(2,1)S(1)}, u32[]{:S(2)}, u32[]{:S(2)}) collective-permute-start(bf16[128,128]{1,0:T(8,128)(2,1)S(1)} %get-tuple-element.35.refs_0_.refs_4_), channel_id=1, source_target_pairs={{0,2},{1,3},{2,0},{3,1},{4,6},{5,7},{6,4},{7,5},{8,10},{9,11},{10,... | collective-permute-start | bytes 98312 | tf_op jit(solution)/shard_map/ppermute | solution.py:484
  5.0 6.9 %slice-start.2 = ((s8[6291456]{0:T(1024)(128)(4,1)}), s8[4194304]{0:T(1024)(128)(4,1)S(1)}, s32[]{:S(2)}) async-start(s8[6291456]{0:T(1024)(128)(4,1)} %bitcast.6), calls=%async_computation.2 | async-start | bytes 8388608
  6.9 3.0 %copy-start.4 = (s32[16]{0:T(128)S(1)}, s32[16]{0:T(128)}, u32[]{:S(2)}) copy-start(s32[16]{0:T(128)} %param.17) | copy-start | bytes 196
  6.9 5.0 %slice-start.3 = ((s8[6291456]{0:T(1024)(128)(4,1)}), s8[2097152]{0:T(1024)(128)(4,1)S(1)}, s32[]{:S(2)}) async-start(s8[6291456]{0:T(1024)(128)(4,1)} %bitcast.6), calls=%async_computation.3 | async-start | bytes 4194304
  6.9 5.0 %copy-start.2 = (bf16[496,1024]{1,0:T(8,128)(2,1)S(1)}, bf16[496,1024]{1,0:T(8,128)(2,1)}, u32[]{:S(2)}) copy-start(bf16[496,1024]{1,0:T(8,128)(2,1)} %refs_4_.1) | copy-start | bytes 3047428
  6.9 11.7 %slice-start = ((s8[8388608]{0:T(1024)(128)(4,1)}), s8[4194304]{0:T(1024)(128)(4,1)S(1)}, s32[]{:S(2)}) async-start(s8[8388608]{0:T(1024)(128)(4,1)} %bitcast.1), calls=%async_computation | async-start | bytes 8388608
  7.0 4.8 %collective-permute-start.1 = (bf16[1024,128]{1,0:T(8,128)(2,1)S(1)}, bf16[1024,128]{1,0:T(8,128)(2,1)S(1)}, u32[]{:S(2)}, u32[]{:S(2)}) collective-permute-start(bf16[1024,128]{1,0:T(8,128)(2,1)S(1)} %get-tuple-element.37), channel_id=1, source_target_pairs={{0,1},{1,0},{2,3},{3,2},{4,5},{5,4},{6,7},{7,6},{8,9},{9,8},{10,11... | collective-permute-start | bytes 786440 | tf_op jit(solution)/shard_map/ppermute | solution.py:484
  7.1 11.5 %collective-permute-start.5 = (bf16[512,128]{1,0:T(8,128)(2,1)S(1)}, bf16[512,128]{1,0:T(8,128)(2,1)S(1)}, u32[]{:S(2)}, u32[]{:S(2)}) collective-permute-start(bf16[512,128]{1,0:T(8,128)(2,1)S(1)} %get-tuple-element.45), channel_id=1, source_target_pairs={{0,2},{1,3},{2,0},{3,1},{4,6},{5,7},{6,4},{7,5},{8,10},{9,11},{10,... | collective-permute-start | bytes 393224 | tf_op jit(solution)/shard_map/ppermute | solution.py:484
  9.2 9.5 %collective-permute-start.6 = (bf16[512,128]{1,0:T(8,128)(2,1)S(1)}, bf16[512,128]{1,0:T(8,128)(2,1)S(1)}, u32[]{:S(2)}, u32[]{:S(2)}) collective-permute-start(bf16[512,128]{1,0:T(8,128)(2,1)S(1)} %get-tuple-element.46), channel_id=1, source_target_pairs={{0,3},{1,2},{2,1},{3,0},{4,7},{5,6},{6,5},{7,4},{8,11},{9,10},{10,... | collective-permute-start | bytes 393224 | tf_op jit(solution)/shard_map/ppermute | solution.py:484
  9.9 7.8 %collective-permute-start.7 = (bf16[256,128]{1,0:T(8,128)(2,1)S(1)}, bf16[256,128]{1,0:T(8,128)(2,1)S(1)}, u32[]{:S(2)}, u32[]{:S(2)}) collective-permute-start(bf16[256,128]{1,0:T(8,128)(2,1)S(1)} %get-tuple-element.48), channel_id=1, source_target_pairs={{0,2},{1,3},{2,0},{3,1},{4,6},{5,7},{6,4},{7,5},{8,10},{9,11},{10,... | collective-permute-start | bytes 196616 | tf_op jit(solution)/shard_map/ppermute | solution.py:484
  11.8 6.8 %slice-start.1 = ((s8[8388608]{0:T(1024)(128)(4,1)}), s8[4194304]{0:T(1024)(128)(4,1)S(1)}, s32[]{:S(2)}) async-start(s8[8388608]{0:T(1024)(128)(4,1)} %bitcast.1), calls=%async_computation.1 | async-start | bytes 8388608
  11.8 6.8 %collective-permute-start.8 = (bf16[256,128]{1,0:T(8,128)(2,1)S(1)}, bf16[256,128]{1,0:T(8,128)(2,1)S(1)}, u32[]{:S(2)}, u32[]{:S(2)}) collective-permute-start(bf16[256,128]{1,0:T(8,128)(2,1)S(1)} %get-tuple-element.49), channel_id=1, source_target_pairs={{0,3},{1,2},{2,1},{3,0},{4,7},{5,6},{6,5},{7,4},{8,11},{9,10},{10,... | collective-permute-start | bytes 196616 | tf_op jit(solution)/shard_map/ppermute | solution.py:484
  26.2 3.3 %collective-permute-start.2 = (bf16[152,128]{1,0:T(8,128)(2,1)S(1)}, bf16[152,128]{1,0:T(8,128)(2,1)S(1)}, u32[]{:S(2)}, u32[]{:S(2)}) collective-permute-start(bf16[152,128]{1,0:T(8,128)(2,1)S(1)} %get-tuple-element.40), channel_id=1, source_target_pairs={{0,1},{1,0},{2,3},{3,2},{4,5},{5,4},{6,7},{7,6},{8,9},{9,8},{10,11... | collective-permute-start | bytes 116744 | tf_op jit(solution)/shard_map/ppermute | solution.py:484
  26.3 4.0 %collective-permute-start.3 = (bf16[152,128]{1,0:T(8,128)(2,1)S(1)}, bf16[152,128]{1,0:T(8,128)(2,1)S(1)}, u32[]{:S(2)}, u32[]{:S(2)}) collective-permute-start(bf16[152,128]{1,0:T(8,128)(2,1)S(1)} %get-tuple-element.41), channel_id=1, source_target_pairs={{0,2},{1,3},{2,0},{3,1},{4,6},{5,7},{6,4},{7,5},{8,10},{9,11},{10,... | collective-permute-start | bytes 116744 | tf_op jit(solution)/shard_map/ppermute | solution.py:484
  28.0 3.8 %collective-permute-start.4 = (bf16[152,128]{1,0:T(8,128)(2,1)S(1)}, bf16[152,128]{1,0:T(8,128)(2,1)S(1)}, u32[]{:S(2)}, u32[]{:S(2)}) collective-permute-start(bf16[152,128]{1,0:T(8,128)(2,1)S(1)} %get-tuple-element.42), channel_id=1, source_target_pairs={{0,3},{1,2},{2,1},{3,0},{4,7},{5,6},{6,5},{7,4},{8,11},{9,10},{10,... | collective-permute-start | bytes 116744 | tf_op jit(solution)/shard_map/ppermute | solution.py:484
  28.1 36.3 %collective-permute-start.13 = (bf16[64,4096]{1,0:T(8,128)(2,1)S(1)}, bf16[64,4096]{1,0:T(8,128)(2,1)S(1)}, u32[]{:S(2)}, u32[]{:S(2)}) collective-permute-start(bf16[64,4096]{1,0:T(8,128)(2,1)S(1)} %get-tuple-element.57), channel_id=1, source_target_pairs={{0,1},{1,0},{2,3},{3,2},{4,5},{5,4},{6,7},{7,6},{8,9},{9,8},{10,11... | collective-permute-start | bytes 1572872 | tf_op jit(solution)/shard_map/ppermute | solution.py:484
  28.5 15.3 %collective-permute-start.14 = (bf16[64,1536]{1,0:T(8,128)(2,1)S(1)}, bf16[64,1536]{1,0:T(8,128)(2,1)S(1)}, u32[]{:S(2)}, u32[]{:S(2)}) collective-permute-start(bf16[64,1536]{1,0:T(8,128)(2,1)S(1)} %get-tuple-element.59), channel_id=1, source_target_pairs={{0,1},{1,0},{2,3},{3,2},{4,5},{5,4},{6,7},{7,6},{8,9},{9,8},{10,11... | collective-permute-start | bytes 589832 | tf_op jit(solution)/shard_map/ppermute | solution.py:484
  29.5 11.8 %collective-permute-start.16 = (bf16[64,2560]{1,0:T(8,128)(2,1)S(1)}, bf16[64,2560]{1,0:T(8,128)(2,1)S(1)}, u32[]{:S(2)}, u32[]{:S(2)}) collective-permute-start(bf16[64,2560]{1,0:T(8,128)(2,1)S(1)} %get-tuple-element.63), channel_id=1, source_target_pairs={{0,1},{1,0},{2,3},{3,2},{4,5},{5,4},{6,7},{7,6},{8,9},{9,8},{10,11... | collective-permute-start | bytes 983048 | tf_op jit(solution)/shard_map/ppermute | solution.py:484
  36.9 27.4 %copy-start = (bf16[128,4096]{1,0:T(8,128)(2,1)S(1)}, bf16[128,4096]{1,0:T(8,128)(2,1)}, u32[]{:S(2)}) copy-start(bf16[128,4096]{1,0:T(8,128)(2,1)} %res_ref.5) | copy-start | bytes 3145732
  36.9 27.4 %copy-start.1 = (f32[4096]{0:T(1024)S(1)}, f32[4096]{0:T(1024)}, u32[]{:S(2)}) copy-start(f32[4096]{0:T(1024)} %param.21) | copy-start | bytes 49156
  36.9 28.8 %collective-permute-start.9 = (bf16[64,4096]{1,0:T(8,128)(2,1)S(1)}, bf16[64,4096]{1,0:T(8,128)(2,1)S(1)}, u32[]{:S(2)}, u32[]{:S(2)}) collective-permute-start(bf16[64,4096]{1,0:T(8,128)(2,1)S(1)} %get-tuple-element.53), channel_id=1, source_target_pairs={{0,1},{1,0},{2,3},{3,2},{4,5},{5,4},{6,7},{7,6},{8,9},{9,8},{10,11... | collective-permute-start | bytes 1572872 | tf_op jit(solution)/shard_map/ppermute | solution.py:484
  40.9 2.0 %collective-permute-start.10 = (bf16[64,4096]{1,0:T(8,128)(2,1)S(1)}, bf16[64,4096]{1,0:T(8,128)(2,1)S(1)}, u32[]{:S(2)}, u32[]{:S(2)}) collective-permute-start(bf16[64,4096]{1,0:T(8,128)(2,1)S(1)} %get-tuple-element.55), channel_id=1, source_target_pairs={{0,1},{1,0},{2,3},{3,2},{4,5},{5,4},{6,7},{7,6},{8,9},{9,8},{10,11... | collective-permute-start | bytes 1572872 | tf_op jit(solution)/shard_map/ppermute | solution.py:484
  41.4 22.9 %collective-permute-start.17 = (bf16[64,2560]{1,0:T(8,128)(2,1)S(1)}, bf16[64,2560]{1,0:T(8,128)(2,1)S(1)}, u32[]{:S(2)}, u32[]{:S(2)}) collective-permute-start(bf16[64,2560]{1,0:T(8,128)(2,1)S(1)} %add_convert_fusion.1), channel_id=1, source_target_pairs={{0,2},{1,3},{2,0},{3,1},{4,6},{5,7},{6,4},{7,5},{8,10},{9,11},{10,... | collective-permute-start | bytes 983048 | tf_op jit(solution)/shard_map/ppermute | solution.py:484
  43.0 22.7 %collective-permute-start.12 = (bf16[48,4096]{1,0:T(8,128)(2,1)S(1)}, bf16[48,4096]{1,0:T(8,128)(2,1)S(1)}, u32[]{:S(2)}, u32[]{:S(2)}) collective-permute-start(bf16[48,4096]{1,0:T(8,128)(2,1)S(1)} %slice.11), channel_id=1, source_target_pairs={{0,2},{1,3},{2,0},{3,1},{4,6},{5,7},{6,4},{7,5},{8,10},{9,11},{10,... | collective-permute-start | bytes 1179656 | tf_op jit(solution)/shard_map/ppermute | solution.py:484
  43.8 20.1 %collective-permute-start.15 = (bf16[64,1536]{1,0:T(8,128)(2,1)S(1)}, bf16[64,1536]{1,0:T(8,128)(2,1)S(1)}, u32[]{:S(2)}, u32[]{:S(2)}) collective-permute-start(bf16[64,1536]{1,0:T(8,128)(2,1)S(1)} %add_convert_fusion.2), channel_id=1, source_target_pairs={{0,2},{1,3},{2,0},{3,1},{4,6},{5,7},{6,4},{7,5},{8,10},{9,11},{10,... | collective-permute-start | bytes 589832 | tf_op jit(solution)/shard_map/ppermute | solution.py:484
  63.8 5.0 %collective-permute-start.11 = (bf16[16,4096]{1,0:T(8,128)(2,1)S(1)}, bf16[16,4096]{1,0:T(8,128)(2,1)S(1)}, u32[]{:S(2)}, u32[]{:S(2)}) collective-permute-start(bf16[16,4096]{1,0:T(8,128)(2,1)S(1)} %slice.10), channel_id=1, source_target_pairs={{0,2},{1,3},{2,0},{3,1},{4,6},{5,7},{6,4},{7,5},{8,10},{9,11},{10,... | collective-permute-start | bytes 393224 | tf_op jit(solution)/shard_map/ppermute | solution.py:484

commit v2 on v1

--- a/solution.py
+++ b/solution.py
@@ -79,12 +79,16 @@
             copy.start()
         for copy in copies:
             copy.wait()
-
+        for o_ref, size in zip(o_refs, sizes):
+            if size > 2 * h_rows:
+                o_ref[2 * h_rows :, :] = q_ref[...]
+
+    sizes = [2 * h_rows + (rows * local_heads if k and k % 2 == 0 else 0) for k in slots]
     outs = pl.pallas_call(
         body,
         in_specs=[in_hbm()] * 3,
         out_specs=[in_vmem()] * (devices + 2),
-        out_shape=[jax.ShapeDtypeStruct((2 * h_rows, HEAD_DIM), BF16)] * devices
+        out_shape=[jax.ShapeDtypeStruct((size, HEAD_DIM), BF16) for size in sizes]
         + [
             jax.ShapeDtypeStruct((rows * local_heads, HEAD_DIM), BF16),
             pltpu.VMEM((2, rows, HEAD_DIM), BF16),
@@ -120,7 +124,8 @@
                 o_refs[i][row + part * p_pad : row + (part + 1) * p_pad, :] = fresh
         row = 2 * (h_rows + p_pad)
         for i, q_ref in enumerate(q_refs):
-            o_refs[0][row + i * q_rows : row + (i + 1) * q_rows, :] = q_ref[...]
+            last = q_ref.shape[0]
+            o_refs[0][row + i * q_rows : row + (i + 1) * q_rows, :] = q_ref[last - q_rows : last, :]
 
     sizes = [2 * (h_rows + p_pad) + len(queries) * q_rows] + [2 * p_pad] * len(slots)
     outs = pl.pallas_call(
@@ -162,8 +167,8 @@
         q_ref[0:prompt_rows, :] = pq_ref[...]
         q_ref[prompt_rows:, :] = jnp.zeros((rows, local_width), BF16)
         for k in range(devices):
-            base = bundle.shape[0] - (devices // 2 - k // 2) * part_rows if k % 2 else 0
             q_ref_k = bundle_ref if k % 2 else q_refs[k // 2]
+            base = q_ref_k.shape[0] - ((devices // 2 - k // 2) if k % 2 else 1) * part_rows
             for h in range(local_heads):
                 row = base + h * rows
                 q_all[k, pl.ds(h, rows, stride=local_heads), :] = q_ref_k[row : row + rows, :].astype(F32)
@@ -490,8 +495,8 @@
     packed, own_query, entries = pack_history(
         history_cache, decode_queries, decode_entries, [1] + slots, local_heads, group
     )
-    even_queries = [own_query] + [swap(own_query, k) for k in range(2, devices, 2)]
     history = {k: swap(packed[k], k) if k else packed[k] for k in slots}
+    even_queries = [own_query] + [history[k] for k in range(2, devices, 2)]
     limits = jnp.concatenate([prompt_start, decode_lengths])
     limits = jnp.broadcast_to(limits[:, None], (limits.shape[0], HEAD_DIM))
     bundle, packed = pack_fresh(prompt_entries, packed[1], even_queries, slots, local_heads, group)

time: 70 us -> 69.2 us (0.989)
    ppermute x18 -> x17, starting transfers between devices: 13.8 us -> 13.2 us  [swap(): return lax.ppermute(value, 'tp', [(i, i ^ k) for i in range(devices)])]
    ppermute x18 -> x17, waiting for transfers between devices: 30.2 us -> 29.8 us  [swap(): return lax.ppermute(value, 'tp', [(i, i ^ k) for i in range(devices)])]
  transfers between devices with their start and end apart: 18 -> 17, of which waited for: 8 -> 8; matrix products, arithmetic and copies ran while one was open for 1% -> 1% of each run, Pallas kernels for 20% -> 20%
where the time goes in v2:
time: 69.2 us; the launch traced here: 69 us
  waiting for transfers between devices  29.8 us (43%)
  Pallas kernels  23.7 us (34%)
  starting transfers between devices  13.2 us (19%)
  between operations  1.8 us (3%)
    ppermute x17, waiting for transfers between devices, swap(): return lax.ppermute(value, 'tp', [(i, i ^ k) for i in range(devices)])  29.8 us
    pallas_call x5, Pallas kernels, attend(): pl.pallas_call(body, in_specs=[in_vmem()] * len(operands), out_specs=[in_...  15.1 us
    ppermute x17, starting transfers between devices, swap(): return lax.ppermute(value, 'tp', [(i, i ^ k) for i in range(devices)])  13.2 us
    pallas_call x3, Pallas kernels, finish(): pl.pallas_call(body, in_specs=[in_vmem()] * n_in + [hbm()] * len(previous...  3.45 us
    pallas_call x1, Pallas kernels, decode_partials(): pl.pallas_call(body, in_specs=[in_vmem()] * (devices // 2 + 4), out_specs...  1.75 us
  transfers between devices with their start and end apart: 17, of which 8 were waited for; matrix products, arithmetic and copies ran while one was open for 1% of the time, Pallas kernels for 20%

profile of v2, /device:TPU:0, one launch (start us, length us, event | category | flops | bytes accessed | tf_op | source)
XLA Modules:
  0.0 69.0 jit_solution(10038714014334936259)
XLA Ops:
  0.6 1.3 %pack_history.1 = (bf16[512,128]{1,0:T(8,128)(2,1)S(1)}, bf16[512,128]{1,0:T(8,128)(2,1)S(1)}, bf16[640,128]{1,0:T(8,128)(2,1)S(1)}, bf16[512,128]{1,0:T(8,128)(...) custom-call(bf16[2,256,512]{2,1,0:T(8,128)(2,1)} %h_hbm.1, bf16[16,1024]{1,0:T(8,128)(2,1)} %q_hbm.1, ...), custom_call_target="tpu_custom_call" | custom-call | flops 3000000000 | bytes 6000000 | tf_op jit(solution)/shard_map/pack_history/pallas_call | solution.py:87
  2.0 3.1 %collective-permute-start = (bf16[640,128]{1,0:T(8,128)(2,1)S(1)}, bf16[640,128]{1,0:T(8,128)(2,1)S(1)}, u32[]{:S(2)}, u32[]{:S(2)}) collective-permute-start(bf16[640,128]{1,0:T(8,128)(2,1)S(1)} %get-tuple-element.36), channel_id=1, source_target_pairs={{0,2},{1,3},{2,0},{3,1},{4,6},{5,7},{6,4},{7,5},{8,10},{9,11},{10,... | collective-permute-start | bytes 491528 | tf_op jit(solution)/shard_map/ppermute | solution.py:489
  5.1 4.2 %collective-permute-done.refs_1_.refs_2_ = bf16[640,128]{1,0:T(8,128)(2,1)S(1)} collective-permute-done((bf16[640,128]{1,0:T(8,128)(2,1)S(1)}, bf16[640,128]{1,0:T(8,128)(2,1)S(1)}, u32[]{:S(2)}, u32[]{:S(2)}) %collective-permute-start) | collective-permute-done | bytes 163872 | tf_op jit(solution)/shard_map/ppermute | solution.py:489
  9.4 1.8 %collective-permute-start.5 = (bf16[512,128]{1,0:T(8,128)(2,1)S(1)}, bf16[512,128]{1,0:T(8,128)(2,1)S(1)}, u32[]{:S(2)}, u32[]{:S(2)}) collective-permute-start(bf16[512,128]{1,0:T(8,128)(2,1)S(1)} %get-tuple-element.46), channel_id=1, source_target_pairs={{0,3},{1,2},{2,1},{3,0},{4,7},{5,6},{6,5},{7,4},{8,11},{9,10},{10,... | collective-permute-start | bytes 393224 | tf_op jit(solution)/shard_map/ppermute | solution.py:489
  12.1 0.4 collective-permute-start.6
  12.6 0.9 %collective-permute-start.7 = (bf16[256,128]{1,0:T(8,128)(2,1)S(1)}, bf16[256,128]{1,0:T(8,128)(2,1)S(1)}, u32[]{:S(2)}, u32[]{:S(2)}) collective-permute-start(bf16[256,128]{1,0:T(8,128)(2,1)S(1)} %get-tuple-element.49), channel_id=1, source_target_pairs={{0,3},{1,2},{2,1},{3,0},{4,7},{5,6},{6,5},{7,4},{8,11},{9,10},{10,... | collective-permute-start | bytes 196616 | tf_op jit(solution)/shard_map/ppermute | solution.py:489
  13.5 1.7 %decode.1 = (bf16[152,128]{1,0:T(8,128)(2,1)S(1)}, bf16[152,128]{1,0:T(8,128)(2,1)S(1)}, bf16[152,128]{1,0:T(8,128)(2,1)S(1)}, bf16[152,128]{1,0:T(8,128)(2,1)S(1)}, bf16[512,1024]{1,0:T(8,128)(2,1)S(1)}) custom-call(s32[17,128]{1,0:T(8,128)S(1)} %broadcast_in_dim.4.limits_ref, bf16[128,128]{1,0:T(8,128)(2,1)S(1)} %get-tuple-element.35.refs_0_.refs_4_, ...), custom_call_target="tpu_custom_call" | custom-call | flops 6000000000 | bytes 12000000 | tf_op jit(solution)/shard_map/decode/pallas_call | solution.py:213
  15.3 2.0 %collective-permute-done.6.refs_5_ = bf16[256,128]{1,0:T(8,128)(2,1)S(1)} collective-permute-done((bf16[256,128]{1,0:T(8,128)(2,1)S(1)}, bf16[256,128]{1,0:T(8,128)(2,1)S(1)}, u32[]{:S(2)}, u32[]{:S(2)}) %collective-permute-start.6) | collective-permute-done | bytes 65568 | tf_op jit(solution)/shard_map/ppermute | solution.py:489
  17.5 2.0 %shard_map.122 = (bf16[1536,256]{1,0:T(8,128)(2,1)S(1)}, bf16[1536,256]{1,0:T(8,128)(2,1)S(1)}, bf16[64,1536]{1,0:T(8,128)(2,1)S(1)}, bf16[64,1024]{1,0:T(8,128)(2,1)S(1)}) custom-call(s32[17,128]{1,0:T(8,128)S(1)} %broadcast_in_dim.4.limits_ref, bf16[512,1024]{1,0:T(8,128)(2,1)S(1)} %get-tuple-element.39.q, bf16[1024,4096]{1,0:T(8,128)(2,1)S(1)} %bitcast.2, ...), custom_call_target="tpu_custom_call" | custom-call | flops 939524096 | bytes 8388608 | tf_op jit(solution)/shard_map/pallas_call | solution.py:410
  19.5 3.6 %shard_map.125 = (bf16[64,4096]{1,0:T(8,128)(2,1)S(1)}, bf16[64,4096]{1,0:T(8,128)(2,1)S(1)}) custom-call(s32[17,128]{1,0:T(8,128)S(1)} %broadcast_in_dim.4.limits_ref, bf16[512,1024]{1,0:T(8,128)(2,1)S(1)} %get-tuple-element.39.q, bf16[1024,4096]{1,0:T(8,128)(2,1)S(1)} %bitcast.2, bf16[1536,256]{1,0:T(8,128)(2,1)S(1)} %get-tuple-element.50.refs_1_.refs_0_, ...), custom_call_target="tpu_custom_call" | custom-call | flops 1879048192 | bytes 8388608 | tf_op jit(solution)/shard_map/pallas_call | solution.py:410
  23.1 1.9 %shard_map.126 = (bf16[64,1536]{1,0:T(8,128)(2,1)S(1)}, bf16[64,1024]{1,0:T(8,128)(2,1)S(1)}) custom-call(s32[17,128]{1,0:T(8,128)S(1)} %broadcast_in_dim.4.limits_ref, bf16[512,1024]{1,0:T(8,128)(2,1)S(1)} %get-tuple-element.39.q, bf16[1024,4096]{1,0:T(8,128)(2,1)S(1)} %bitcast.2, bf16[1536,256]{1,0:T(8,128)(2,1)S(1)} %get-tuple-element.50.refs_1_.refs_0_, ...), custom_call_target="tpu_custom_call" | custom-call | flops 939524096 | bytes 8388608 | tf_op jit(solution)/shard_map/pallas_call | solution.py:410
  25.0 0.5 collective-permute-start.2
  25.5 1.7 %collective-permute-start.3 = (bf16[152,128]{1,0:T(8,128)(2,1)S(1)}, bf16[152,128]{1,0:T(8,128)(2,1)S(1)}, u32[]{:S(2)}, u32[]{:S(2)}) collective-permute-start(bf16[152,128]{1,0:T(8,128)(2,1)S(1)} %get-tuple-element.42), channel_id=1, source_target_pairs={{0,2},{1,3},{2,0},{3,1},{4,6},{5,7},{6,4},{7,5},{8,10},{9,11},{10,... | collective-permute-start | bytes 116744 | tf_op jit(solution)/shard_map/ppermute | solution.py:489
  27.2 0.4 collective-permute-start.12
  27.7 0.9 %project.1 = (bf16[64,2560]{1,0:T(8,128)(2,1)S(1)}, bf16[64,2560]{1,0:T(8,128)(2,1)S(1)}) custom-call(bf16[64,1024]{1,0:T(8,128)(2,1)S(1)} %get-tuple-element.60.refs_0_, bf16[64,1024]{1,0:T(8,128)(2,1)S(1)} %get-tuple-element.61.refs_1_, bf16[1024,4096]{1,0:T(8,128)(2,1)S(1)} %bitcast.2), custom_call_target="tpu_custom_call" | custom-call | flops 1000000000 | bytes 2000000 | tf_op jit(solution)/shard_map/project/pallas_call | solution.py:294
  28.6 0.5 collective-permute-start.15
  29.1 0.4 collective-permute-done.3.refs_2_
  29.5 1.5 %collective-permute-done.4.refs_3_ = bf16[152,128]{1,0:T(8,128)(2,1)S(1)} collective-permute-done((bf16[152,128]{1,0:T(8,128)(2,1)S(1)}, bf16[152,128]{1,0:T(8,128)(2,1)S(1)}, u32[]{:S(2)}, u32[]{:S(2)}) %collective-permute-start.4) | collective-permute-done | bytes 38944 | tf_op jit(solution)/shard_map/ppermute | solution.py:489
  31.0 1.2 %join.1.refs_0_ = bf16[16,1024]{1,0:T(8,128)(2,1)S(1)} custom-call(bf16[152,128]{1,0:T(8,128)(2,1)S(1)} %get-tuple-element.40.refs_0_, bf16[152,128]{1,0:T(8,128)(2,1)S(1)} %collective-permute-done.2.refs_1_, bf16[152,128]{1,0:T(8,128)(2,1)S(1)} %collective-permute-done.3.refs_2_, bf16[152,128]{1,0:T(8,128)(2,1)S(1)} %collective-permute-done.4.refs_3_, ...), custom_call_target="tpu_custom_call" | custom-call | flops 500000000 | bytes 1000000 | tf_op jit(solution)/shard_map/join/pallas_call | solution.py:264
  32.2 3.9 %shard_map.123 = (bf16[64,4096]{1,0:T(8,128)(2,1)S(1)}, bf16[64,4096]{1,0:T(8,128)(2,1)S(1)}) custom-call(s32[17,128]{1,0:T(8,128)S(1)} %broadcast_in_dim.4.limits_ref, bf16[512,1024]{1,0:T(8,128)(2,1)S(1)} %get-tuple-element.39.q, bf16[1024,4096]{1,0:T(8,128)(2,1)S(1)} %bitcast.2, bf16[16,1024]{1,0:T(8,128)(2,1)S(1)} %join.1.refs_0_, ...), custom_call_target="tpu_custom_call" | custom-call | flops 1879048192 | bytes 8388608 | tf_op jit(solution)/shard_map/pallas_call | solution.py:410
  36.3 3.7 %shard_map.124 = (bf16[64,4096]{1,0:T(8,128)(2,1)S(1)}, bf16[64,4096]{1,0:T(8,128)(2,1)S(1)}) custom-call(s32[17,128]{1,0:T(8,128)S(1)} %broadcast_in_dim.4.limits_ref, bf16[512,1024]{1,0:T(8,128)(2,1)S(1)} %get-tuple-element.39.q, bf16[1024,4096]{1,0:T(8,128)(2,1)S(1)} %bitcast.2, bf16[16,1024]{1,0:T(8,128)(2,1)S(1)} %join.1.refs_0_, ...), custom_call_target="tpu_custom_call" | custom-call | flops 1879048192 | bytes 8388608 | tf_op jit(solution)/shard_map/pallas_call | solution.py:410
  40.0 0.5 collective-permute-start.9
  40.6 0.4 collective-permute-start.16
  41.0 1.0 %collective-permute-done.9 = bf16[64,4096]{1,0:T(8,128)(2,1)S(1)} collective-permute-done((bf16[64,4096]{1,0:T(8,128)(2,1)S(1)}, bf16[64,4096]{1,0:T(8,128)(2,1)S(1)}, u32[]{:S(2)}, u32[]{:S(2)}) %collective-permute-start.9) | collective-permute-done | bytes 524320 | tf_op jit(solution)/shard_map/ppermute | solution.py:489
  42.2 0.7 %collective-permute-start.11 = (bf16[48,4096]{1,0:T(8,128)(2,1)S(1)}, bf16[48,4096]{1,0:T(8,128)(2,1)S(1)}, u32[]{:S(2)}, u32[]{:S(2)}) collective-permute-start(bf16[48,4096]{1,0:T(8,128)(2,1)S(1)} %slice.11), channel_id=1, source_target_pairs={{0,2},{1,3},{2,0},{3,1},{4,6},{5,7},{6,4},{7,5},{8,10},{9,11},{10,... | collective-permute-start | bytes 1179656 | tf_op jit(solution)/shard_map/ppermute | solution.py:489
  43.0 1.4 %collective-permute-start.14 = (bf16[64,1536]{1,0:T(8,128)(2,1)S(1)}, bf16[64,1536]{1,0:T(8,128)(2,1)S(1)}, u32[]{:S(2)}, u32[]{:S(2)}) collective-permute-start(bf16[64,1536]{1,0:T(8,128)(2,1)S(1)} %add_convert_fusion.2), channel_id=1, source_target_pairs={{0,2},{1,3},{2,0},{3,1},{4,6},{5,7},{6,4},{7,5},{8,10},{9,11},{10,... | collective-permute-start | bytes 589832 | tf_op jit(solution)/shard_map/ppermute | solution.py:489
  44.4 18.6 %collective-permute-done.14.refs_0_ = bf16[64,1536]{1,0:T(8,128)(2,1)S(1)} collective-permute-done((bf16[64,1536]{1,0:T(8,128)(2,1)S(1)}, bf16[64,1536]{1,0:T(8,128)(2,1)S(1)}, u32[]{:S(2)}, u32[]{:S(2)}) %collective-permute-start.14) | collective-permute-done | bytes 196640 | tf_op jit(solution)/shard_map/ppermute | solution.py:489
  63.0 0.5 collective-permute-start.10
  63.5 1.4 %shard_map.127 = (bf16[128,4096]{1,0:T(8,128)(2,1)}, bf16[128,4096]{1,0:T(8,128)(2,1)}) custom-call(bf16[128,4096]{1,0:T(8,128)(2,1)S(1)} %copy-done, bf16[64,4096]{1,0:T(8,128)(2,1)S(1)} %get-tuple-element.56.own_ref, bf16[64,4096]{1,0:T(8,128)(2,1)S(1)} %collective-permute-done.12.given_ref, bf16[64,1536]{1,0:T(8,128)(2,1)S(1)} %collective-permute-done.14.refs_0_, ...), custom_call_target="tpu_custom_call" | custom-call | flops 1000000000 | bytes 2000000 | tf_op jit(solution)/shard_map/pallas_call | solution.py:454
  64.9 1.2 %shard_map.128 = (bf16[128,4096]{1,0:T(8,128)(2,1)}, bf16[128,4096]{1,0:T(8,128)(2,1)}) custom-call(bf16[128,4096]{1,0:T(8,128)(2,1)S(1)} %copy-done, bf16[64,4096]{1,0:T(8,128)(2,1)S(1)} %get-tuple-element.52.own_ref, bf16[64,4096]{1,0:T(8,128)(2,1)S(1)} %collective-permute-done.8.given_ref, ...), custom_call_target="tpu_custom_call", output_to_operand_aliasing={{0}: (5, {}), {1}: (6, {})} | custom-call | flops 1000000000 | bytes 2000000 | tf_op jit(solution)/shard_map/pallas_call | solution.py:454
  66.1 1.8 %collective-permute-done.10.refs_0_ = bf16[16,4096]{1,0:T(8,128)(2,1)S(1)} collective-permute-done((bf16[16,4096]{1,0:T(8,128)(2,1)S(1)}, bf16[16,4096]{1,0:T(8,128)(2,1)S(1)}, u32[]{:S(2)}, u32[]{:S(2)}) %collective-permute-start.10) | collective-permute-done | bytes 131104 | tf_op jit(solution)/shard_map/ppermute | solution.py:489
  68.0 0.9 %shard_map.129 = (bf16[128,4096]{1,0:T(8,128)(2,1)}, bf16[128,4096]{1,0:T(8,128)(2,1)}) custom-call(bf16[128,4096]{1,0:T(8,128)(2,1)S(1)} %copy-done, bf16[64,4096]{1,0:T(8,128)(2,1)S(1)} %get-tuple-element.52.own_ref, bf16[64,4096]{1,0:T(8,128)(2,1)S(1)} %collective-permute-done.8.given_ref, ...), custom_call_target="tpu_custom_call", output_to_operand_aliasing={{0}: (5, {}), {1}: (6, {})} | custom-call | flops 1000000000 | bytes 2000000 | tf_op jit(solution)/shard_map/pallas_call | solution.py:454
  (43 shorter events, 1.1 us)
Async XLA Ops:
  0.6 4.4 %copy-start.3 = (bf16[2,124,512]{2,0,1:T(2,128)(2,1)S(1)}, bf16[2,124,512]{2,0,1:T(2,128)(2,1)}, u32[]{:S(2)}) copy-start(bf16[2,124,512]{2,0,1:T(2,128)(2,1)} %param.12) | copy-start | bytes 761860
  2.0 7.3 %collective-permute-start = (bf16[640,128]{1,0:T(8,128)(2,1)S(1)}, bf16[640,128]{1,0:T(8,128)(2,1)S(1)}, u32[]{:S(2)}, u32[]{:S(2)}) collective-permute-start(bf16[640,128]{1,0:T(8,128)(2,1)S(1)} %get-tuple-element.36), channel_id=1, source_target_pairs={{0,2},{1,3},{2,0},{3,1},{4,6},{5,7},{6,4},{7,5},{8,10},{9,11},{10,... | collective-permute-start | bytes 491528 | tf_op jit(solution)/shard_map/ppermute | solution.py:489
  5.0 8.5 %slice-start.2 = ((s8[6291456]{0:T(1024)(128)(4,1)}), s8[4194304]{0:T(1024)(128)(4,1)S(1)}, s32[]{:S(2)}) async-start(s8[6291456]{0:T(1024)(128)(4,1)} %bitcast.6), calls=%async_computation.2 | async-start | bytes 8388608
  9.2 2.8 %copy-start.4 = (s32[16]{0:T(128)S(1)}, s32[16]{0:T(128)}, u32[]{:S(2)}) copy-start(s32[16]{0:T(128)} %param.17) | copy-start | bytes 196
  9.2 4.3 %slice-start.3 = ((s8[6291456]{0:T(1024)(128)(4,1)}), s8[2097152]{0:T(1024)(128)(4,1)S(1)}, s32[]{:S(2)}) async-start(s8[6291456]{0:T(1024)(128)(4,1)} %bitcast.6), calls=%async_computation.3 | async-start | bytes 4194304
  9.2 4.3 %copy-start.2 = (bf16[496,1024]{1,0:T(8,128)(2,1)S(1)}, bf16[496,1024]{1,0:T(8,128)(2,1)}, u32[]{:S(2)}) copy-start(bf16[496,1024]{1,0:T(8,128)(2,1)} %refs_4_.1) | copy-start | bytes 3047428
  9.2 8.3 %slice-start = ((s8[8388608]{0:T(1024)(128)(4,1)}), s8[4194304]{0:T(1024)(128)(4,1)S(1)}, s32[]{:S(2)}) async-start(s8[8388608]{0:T(1024)(128)(4,1)} %bitcast.1), calls=%async_computation | async-start | bytes 8388608
  9.3 4.1 %collective-permute-start.1 = (bf16[1024,128]{1,0:T(8,128)(2,1)S(1)}, bf16[1024,128]{1,0:T(8,128)(2,1)S(1)}, u32[]{:S(2)}, u32[]{:S(2)}) collective-permute-start(bf16[1024,128]{1,0:T(8,128)(2,1)S(1)} %get-tuple-element.38), channel_id=1, source_target_pairs={{0,1},{1,0},{2,3},{3,2},{4,5},{5,4},{6,7},{7,6},{8,9},{9,8},{10,11... | collective-permute-start | bytes 786440 | tf_op jit(solution)/shard_map/ppermute | solution.py:489
  9.4 5.9 %collective-permute-start.5 = (bf16[512,128]{1,0:T(8,128)(2,1)S(1)}, bf16[512,128]{1,0:T(8,128)(2,1)S(1)}, u32[]{:S(2)}, u32[]{:S(2)}) collective-permute-start(bf16[512,128]{1,0:T(8,128)(2,1)S(1)} %get-tuple-element.46), channel_id=1, source_target_pairs={{0,3},{1,2},{2,1},{3,0},{4,7},{5,6},{6,5},{7,4},{8,11},{9,10},{10,... | collective-permute-start | bytes 393224 | tf_op jit(solution)/shard_map/ppermute | solution.py:489
  12.1 5.2 %collective-permute-start.6 = (bf16[256,128]{1,0:T(8,128)(2,1)S(1)}, bf16[256,128]{1,0:T(8,128)(2,1)S(1)}, u32[]{:S(2)}, u32[]{:S(2)}) collective-permute-start(bf16[256,128]{1,0:T(8,128)(2,1)S(1)} %get-tuple-element.48), channel_id=1, source_target_pairs={{0,2},{1,3},{2,0},{3,1},{4,6},{5,7},{6,4},{7,5},{8,10},{9,11},{10,... | collective-permute-start | bytes 196616 | tf_op jit(solution)/shard_map/ppermute | solution.py:489
  12.5 5.0 %slice-start.1 = ((s8[8388608]{0:T(1024)(128)(4,1)}), s8[4194304]{0:T(1024)(128)(4,1)S(1)}, s32[]{:S(2)}) async-start(s8[8388608]{0:T(1024)(128)(4,1)} %bitcast.1), calls=%async_computation.1 | async-start | bytes 8388608
  12.6 5.0 %collective-permute-start.7 = (bf16[256,128]{1,0:T(8,128)(2,1)S(1)}, bf16[256,128]{1,0:T(8,128)(2,1)S(1)}, u32[]{:S(2)}, u32[]{:S(2)}) collective-permute-start(bf16[256,128]{1,0:T(8,128)(2,1)S(1)} %get-tuple-element.49), channel_id=1, source_target_pairs={{0,3},{1,2},{2,1},{3,0},{4,7},{5,6},{6,5},{7,4},{8,11},{9,10},{10,... | collective-permute-start | bytes 196616 | tf_op jit(solution)/shard_map/ppermute | solution.py:489
  25.0 3.6 %collective-permute-start.2 = (bf16[152,128]{1,0:T(8,128)(2,1)S(1)}, bf16[152,128]{1,0:T(8,128)(2,1)S(1)}, u32[]{:S(2)}, u32[]{:S(2)}) collective-permute-start(bf16[152,128]{1,0:T(8,128)(2,1)S(1)} %get-tuple-element.41), channel_id=1, source_target_pairs={{0,1},{1,0},{2,3},{3,2},{4,5},{5,4},{6,7},{7,6},{8,9},{9,8},{10,11... | collective-permute-start | bytes 116744 | tf_op jit(solution)/shard_map/ppermute | solution.py:489
  25.5 4.0 %collective-permute-start.3 = (bf16[152,128]{1,0:T(8,128)(2,1)S(1)}, bf16[152,128]{1,0:T(8,128)(2,1)S(1)}, u32[]{:S(2)}, u32[]{:S(2)}) collective-permute-start(bf16[152,128]{1,0:T(8,128)(2,1)S(1)} %get-tuple-element.42), channel_id=1, source_target_pairs={{0,2},{1,3},{2,0},{3,1},{4,6},{5,7},{6,4},{7,5},{8,10},{9,11},{10,... | collective-permute-start | bytes 116744 | tf_op jit(solution)/shard_map/ppermute | solution.py:489
  27.2 3.8 %collective-permute-start.4 = (bf16[152,128]{1,0:T(8,128)(2,1)S(1)}, bf16[152,128]{1,0:T(8,128)(2,1)S(1)}, u32[]{:S(2)}, u32[]{:S(2)}) collective-permute-start(bf16[152,128]{1,0:T(8,128)(2,1)S(1)} %get-tuple-element.43), channel_id=1, source_target_pairs={{0,3},{1,2},{2,1},{3,0},{4,7},{5,6},{6,5},{7,4},{8,11},{9,10},{10,... | collective-permute-start | bytes 116744 | tf_op jit(solution)/shard_map/ppermute | solution.py:489
  27.2 36.3 %collective-permute-start.12 = (bf16[64,4096]{1,0:T(8,128)(2,1)S(1)}, bf16[64,4096]{1,0:T(8,128)(2,1)S(1)}, u32[]{:S(2)}, u32[]{:S(2)}) collective-permute-start(bf16[64,4096]{1,0:T(8,128)(2,1)S(1)} %get-tuple-element.57), channel_id=1, source_target_pairs={{0,1},{1,0},{2,3},{3,2},{4,5},{5,4},{6,7},{7,6},{8,9},{9,8},{10,11... | collective-permute-start | bytes 1572872 | tf_op jit(solution)/shard_map/ppermute | solution.py:489
  27.6 15.3 %collective-permute-start.13 = (bf16[64,1536]{1,0:T(8,128)(2,1)S(1)}, bf16[64,1536]{1,0:T(8,128)(2,1)S(1)}, u32[]{:S(2)}, u32[]{:S(2)}) collective-permute-start(bf16[64,1536]{1,0:T(8,128)(2,1)S(1)} %get-tuple-element.59), channel_id=1, source_target_pairs={{0,1},{1,0},{2,3},{3,2},{4,5},{5,4},{6,7},{7,6},{8,9},{9,8},{10,11... | collective-permute-start | bytes 589832 | tf_op jit(solution)/shard_map/ppermute | solution.py:489
  28.6 11.9 %collective-permute-start.15 = (bf16[64,2560]{1,0:T(8,128)(2,1)S(1)}, bf16[64,2560]{1,0:T(8,128)(2,1)S(1)}, u32[]{:S(2)}, u32[]{:S(2)}) collective-permute-start(bf16[64,2560]{1,0:T(8,128)(2,1)S(1)} %get-tuple-element.63), channel_id=1, source_target_pairs={{0,1},{1,0},{2,3},{3,2},{4,5},{5,4},{6,7},{7,6},{8,9},{9,8},{10,11... | collective-permute-start | bytes 983048 | tf_op jit(solution)/shard_map/ppermute | solution.py:489
  36.1 27.4 %copy-start = (bf16[128,4096]{1,0:T(8,128)(2,1)S(1)}, bf16[128,4096]{1,0:T(8,128)(2,1)}, u32[]{:S(2)}) copy-start(bf16[128,4096]{1,0:T(8,128)(2,1)} %res_ref.5) | copy-start | bytes 3145732
  36.1 27.4 %copy-start.1 = (f32[4096]{0:T(1024)S(1)}, f32[4096]{0:T(1024)}, u32[]{:S(2)}) copy-start(f32[4096]{0:T(1024)} %param.21) | copy-start | bytes 49156
  36.1 28.8 %collective-permute-start.8 = (bf16[64,4096]{1,0:T(8,128)(2,1)S(1)}, bf16[64,4096]{1,0:T(8,128)(2,1)S(1)}, u32[]{:S(2)}, u32[]{:S(2)}) collective-permute-start(bf16[64,4096]{1,0:T(8,128)(2,1)S(1)} %get-tuple-element.53), channel_id=1, source_target_pairs={{0,1},{1,0},{2,3},{3,2},{4,5},{5,4},{6,7},{7,6},{8,9},{9,8},{10,11... | collective-permute-start | bytes 1572872 | tf_op jit(solution)/shard_map/ppermute | solution.py:489
  40.0 2.0 %collective-permute-start.9 = (bf16[64,4096]{1,0:T(8,128)(2,1)S(1)}, bf16[64,4096]{1,0:T(8,128)(2,1)S(1)}, u32[]{:S(2)}, u32[]{:S(2)}) collective-permute-start(bf16[64,4096]{1,0:T(8,128)(2,1)S(1)} %get-tuple-element.55), channel_id=1, source_target_pairs={{0,1},{1,0},{2,3},{3,2},{4,5},{5,4},{6,7},{7,6},{8,9},{9,8},{10,11... | collective-permute-start | bytes 1572872 | tf_op jit(solution)/shard_map/ppermute | solution.py:489
  40.6 22.9 %collective-permute-start.16 = (bf16[64,2560]{1,0:T(8,128)(2,1)S(1)}, bf16[64,2560]{1,0:T(8,128)(2,1)S(1)}, u32[]{:S(2)}, u32[]{:S(2)}) collective-permute-start(bf16[64,2560]{1,0:T(8,128)(2,1)S(1)} %add_convert_fusion.1), channel_id=1, source_target_pairs={{0,2},{1,3},{2,0},{3,1},{4,6},{5,7},{6,4},{7,5},{8,10},{9,11},{10,... | collective-permute-start | bytes 983048 | tf_op jit(solution)/shard_map/ppermute | solution.py:489
  42.2 22.7 %collective-permute-start.11 = (bf16[48,4096]{1,0:T(8,128)(2,1)S(1)}, bf16[48,4096]{1,0:T(8,128)(2,1)S(1)}, u32[]{:S(2)}, u32[]{:S(2)}) collective-permute-start(bf16[48,4096]{1,0:T(8,128)(2,1)S(1)} %slice.11), channel_id=1, source_target_pairs={{0,2},{1,3},{2,0},{3,1},{4,6},{5,7},{6,4},{7,5},{8,10},{9,11},{10,... | collective-permute-start | bytes 1179656 | tf_op jit(solution)/shard_map/ppermute | solution.py:489
  43.0 20.0 %collective-permute-start.14 = (bf16[64,1536]{1,0:T(8,128)(2,1)S(1)}, bf16[64,1536]{1,0:T(8,128)(2,1)S(1)}, u32[]{:S(2)}, u32[]{:S(2)}) collective-permute-start(bf16[64,1536]{1,0:T(8,128)(2,1)S(1)} %add_convert_fusion.2), channel_id=1, source_target_pairs={{0,2},{1,3},{2,0},{3,1},{4,6},{5,7},{6,4},{7,5},{8,10},{9,11},{10,... | collective-permute-start | bytes 589832 | tf_op jit(solution)/shard_map/ppermute | solution.py:489
  63.0 5.0 %collective-permute-start.10 = (bf16[16,4096]{1,0:T(8,128)(2,1)S(1)}, bf16[16,4096]{1,0:T(8,128)(2,1)S(1)}, u32[]{:S(2)}, u32[]{:S(2)}) collective-permute-start(bf16[16,4096]{1,0:T(8,128)(2,1)S(1)} %slice.10), channel_id=1, source_target_pairs={{0,2},{1,3},{2,0},{3,1},{4,6},{5,7},{6,4},{7,5},{8,10},{9,11},{10,... | collective-permute-start | bytes 393224 | tf_op jit(solution)/shard_map/ppermute | solution.py:489
